TPU v7x, 128 devices: a whole 4x4x4 slice. The times are simulated.
128 devices in a mesh: row: 8 (over y_hi, x), col: 16 (over z, y_lo, core).
Axes of the slice: x: 4, y: 4 (y_hi: 2, y_lo: 2; y = y_hi * 2 + y_lo), z: 4, core: 2. Of those that a mesh axis runs over, the one named last changes fastest.
Arguments:
- integrals: bfloat16 [2400, 2400, 256], P('row', 'col'), may hold values from -6 to 6
- occ_coef: bfloat16 [2400, 96], P('row'), may hold values from -0.125 to 0.125
- virt_coef: bfloat16 [2400, 2304], P('col'), may hold values from -0.125 to 0.125
- pair_index: int32 [256], replicated, may hold values from 0 to 255, each once
Outputs:
- transformed: bfloat16 [96, 2304, 256], P('row', 'col')
Inputs may be any that keep to these rules, and one draw needn't show every extreme that they name: pair_index holds each of 0 to 255 once.
All inputs are finite; a program needn't handle non-finite values.
Results may differ from a plain program's by a relative error of at most 0.0049.
Values may be sent and summed in bfloat16 or wider, within the bound.
No kernel may reach another device: no remote copies, remote signals or barrier semaphores. Data moves between devices by JAX's collectives and lax.ppermute only.
A program may use at most 192 MiB of HBM per device.

v0:
```python
import jax
import jax.numpy as jnp
from jax import lax
from jax.sharding import PartitionSpec as P


def local(integrals, occ_coef, virt_coef, pair_index):
    half_rows = lax.psum_scatter(
        jnp.einsum("mi,mnp->inp", occ_coef, integrals, preferred_element_type=jnp.float32),
        "row",
        scatter_dimension=0,
        tiled=True,
    ).astype(jnp.bfloat16)
    virt_cols = lax.all_to_all(virt_coef, "col", split_axis=1, concat_axis=0, tiled=True)
    slab_local = jnp.einsum(
        "inp,na->iap",
        lax.all_gather(half_rows, "col", axis=1, tiled=True),
        virt_cols,
        preferred_element_type=jnp.float32,
    )
    slab_local = slab_local.astype(jnp.bfloat16)
    return jnp.take(slab_local, pair_index, axis=2)


def solution(mesh):
    return jax.shard_map(
        local,
        mesh=mesh,
        in_specs=(P("row", "col", None), P("row", None), P("col", None), P()),
        out_specs=P("row", "col", None),
        check_vma=False,
    )
```

profile of v0, /device:TPU:1, one launch (start us, length us, event | category | flops | bytes accessed | tf_op | source)
XLA Modules:
  0.0 363.8 jit_solution(18338669772870637867)
XLA Ops:
  6.5 0.0 copy-start
  6.5 0.0 reduce-scatter.2.cloned.1.call-start
  6.5 0.9 copy-done
  7.4 14.3 %fusion = f32[96,150,256]{2,0,1:T(8,128)} fusion(bf16[300,150,256]{2,1,0:T(8,128)(2,1)} %param.4, bf16[300,96]{0,1:T(8,128)(2,1)S(1)} %copy-done), kind=kOutput, calls=%fused_computation.1 | convolution fusion | flops 2211840000 | bytes 37843200 | tf_op jit(solution)/shard_map/mi,mnp->inp/dot_general | solution.py:9
  21.7 19.0 %copy.16 = f32[96,150,256]{2,1,0:T(8,128)} copy(f32[96,150,256]{2,0,1:T(8,128)} %fusion) | data formatting | bytes 29491200 | tf_op jit(solution)/shard_map/mi,mnp->inp/dot_general | solution.py:9
  40.7 0.0 reduce-scatter.2.cloned.1.call-update
  40.8 0.0 all-gather.2.cloned.1.call-start
  40.8 174.7 %reduce-scatter.2.cloned.1.call-done = f32[12,150,256]{2,1,0:T(8,128)} async-done(((f32[96,150,256]{2,1,0:T(8,128)}), f32[12,150,256]{2,1,0:T(8,128)}) %reduce-scatter.2.cloned.1.call-update) | async-done | bytes 1843216 | tf_op jit(solution)/shard_map/reduce_scatter | solution.py:8
  215.5 1.6 convert_element_type.9
  217.1 0.0 copy-start.2
  217.1 1.3 copy.17
  218.4 0.0 all-gather.2.cloned.1.call-update
  218.4 0.0 copy-done.2
  218.4 0.0 copy-start.3
  218.4 1.4 copy.23
  219.8 5.9 %all-to-all-start = ((bf16[150,16,144]{0,2,1:T(8,128)(2,1)}), bf16[150,16,144]{0,2,1:T(8,128)(2,1)S(1)}, u32[]{:S(2)}, u32[]{:S(2)}) async-start(bf16[150,16,144]{0,2,1:T(8,128)(2,1)} %bitcast.1), calls=%async_computation.1 | async-start | bytes 2359296 | tf_op jit(solution)/shard_map/all_to_all | solution.py:14
  225.7 0.0 copy-done.3
  225.8 29.2 %all-to-all-done = bf16[150,16,144]{0,2,1:T(8,128)(2,1)S(1)} async-done(((bf16[150,16,144]{0,2,1:T(8,128)(2,1)}), bf16[150,16,144]{0,2,1:T(8,128)(2,1)S(1)}, u32[]{:S(2)}, u32[]{:S(2)}) %all-to-all-start) | async-done | bytes 691232 | tf_op jit(solution)/shard_map/all_to_all | solution.py:14
  255.0 0.4 copy.19
  255.4 1.8 reshape.18
  257.1 78.2 %all-gather.2.cloned.1.call-done = bf16[12,2400,256]{2,0,1:T(8,128)(2,1)} async-done(((bf16[12,150,256]{2,0,1:T(8,128)(2,1)}), bf16[12,2400,256]{2,0,1:T(8,128)(2,1)}) %all-gather.2.cloned.1.call-update) | async-done | bytes 14745616 | tf_op jit(solution)/shard_map/all_gather | solution.py:17
  335.4 11.7 %fusion.7 = bf16[12,144,256]{2,1,0:T(8,128)(2,1)S(1)} fusion(bf16[2400,144,1]{0,1,2:T(8,128)(2,1)S(1)} %reshape.18, bf16[12,2400,256]{2,0,1:T(8,128)(2,1)} %all-gather.2.cloned.1.call-done), kind=kOutput, calls=%fused_computation.7 | convolution fusion | flops 2123808768 | bytes 16321536 | tf_op jit(solution)/shard_map/inp,na->iap/dot_general | solution.py:15
  347.1 3.1 copy.21
  350.2 2.1 gather_fusion
  352.2 0.0 copy-start.1
  352.2 2.2 select_bitcast_fusion
  354.4 2.5 copy.22
  356.9 0.0 copy-done.1
  (3 shorter events, 0.0 us)
Async XLA Ops:
  6.5 0.9 copy-start
  6.5 209.0 %reduce-scatter.2.cloned.1.call-start = ((), (), s32[]{:S(2)}) async-start(), calls=%async_computation.2 | async-start | bytes 16809984 | tf_op jit(solution)/shard_map/reduce_scatter | solution.py:8
  40.8 294.6 %all-gather.2.cloned.1.call-start = ((), (), s32[]{:S(2)}) async-start(), calls=%async_computation.3 | async-start | bytes 20889600 | tf_op jit(solution)/shard_map/all_gather | solution.py:17
  217.1 1.3 copy-start.2
  218.4 7.3 %copy-start.3 = (s32[256]{0:T(256)S(1)}, s32[256]{0:T(256)}, u32[]{:S(2)}) copy-start(s32[256]{0:T(256)} %param.7) | copy-start | bytes 3076
  219.8 35.2 %all-to-all-start = ((bf16[150,16,144]{0,2,1:T(8,128)(2,1)}), bf16[150,16,144]{0,2,1:T(8,128)(2,1)S(1)}, u32[]{:S(2)}, u32[]{:S(2)}) async-start(bf16[150,16,144]{0,2,1:T(8,128)(2,1)} %bitcast.1), calls=%async_computation.1 | async-start | bytes 2359296 | tf_op jit(solution)/shard_map/all_to_all | solution.py:14
  352.2 4.7 %copy-start.1 = (bf16[300,96]{0,1:T(8,128)(2,1)S(1)}, bf16[300,96]{0,1:T(8,128)(2,1)}, u32[]{:S(2)}) copy-start(bf16[300,96]{0,1:T(8,128)(2,1)} %param.5) | copy-start | bytes 172804
Sparse Core Ops, SparseCore 0:
  40.9 174.5 reduce-scatter.1
  218.5 116.8 all-gather.1
where the time goes:
time: 364 us
  waiting for transfers between devices  282 us (77%)
  local copies, waits for them, and re-layouts  32.4 us (9%)
  matrix products  26 us (7%)
  between operations  13.5 us (4%)
  starting transfers between devices  5.92 us (2%)
  other arithmetic  3.79 us (1%)
    reduce_scatter x1, waiting for transfers between devices, local(): lax.psum_scatter(jnp.einsum('mi,mnp->inp', occ_coef, integrals, preferred...  175 us
    all_gather x1, waiting for transfers between devices, local(): lax.all_gather(half_rows, 'col', axis=1, tiled=True)  78.2 us
    all_to_all x1, waiting for transfers between devices, local(): lax.all_to_all(virt_coef, 'col', split_axis=1, concat_axis=0, tiled=True)  29.2 us
    dot_general x1, local copies, waits for them, and re-layouts, local(): jnp.einsum('mi,mnp->inp', occ_coef, integrals, preferred_element_type=jnp...  19 us
    dot_general x1, matrix products, local(): jnp.einsum('mi,mnp->inp', occ_coef, integrals, preferred_element_type=jnp...  14.3 us
    dot_general x1, matrix products, local(): jnp.einsum('inp,na->iap', lax.all_gather(half_rows, 'col', axis=1, tiled=...  11.7 us
  transfers between devices with their start and end apart: 3, of which 3 were waited for; matrix products, arithmetic and copies ran while one was open for 1% of the time, Pallas kernels for 0%

commit v1 on v0

v1 whole, which is shorter than its diff:
```python
import jax
import jax.numpy as jnp
from jax import lax
from jax.sharding import PartitionSpec as P

F32, BF16 = jnp.float32, jnp.bfloat16
O_BLK = 12
A_BLK = 144
CHUNKS = (
    ((0, 40), (40, 80), (0, 256)),
    ((80, 112), (112, 150), (0, 256)),
)


def row_perm(mask):
    return [(i, i ^ mask) for i in range(8)]


def col_xor(mask):
    return [(i, i ^ mask) for i in range(16)]


def col_z(k):
    return [(i, (i + 4 * k) % 16) for i in range(16)]


def select_cols(mat, source):
    hot = (lax.broadcasted_iota(jnp.int32, (mat.shape[1], source.shape[0]), 0) == source[None, :]).astype(BF16)
    return jnp.dot(mat, hot, preferred_element_type=F32).astype(BF16)


def local(integrals, occ_coef, virt_coef, pair_index):
    r = lax.axis_index("row")
    c = lax.axis_index("col")
    yh, x = r // 4, r % 4
    z, yl, core = c // 4, (c // 2) % 2, c % 2

    pos = jnp.arange(96, dtype=jnp.int32)
    slot, j, t = pos // 24, (pos // O_BLK) % 2, pos % O_BLK

    def occ_source(order):
        k = sum(jnp.where(slot == s, order[s], 0) for s in range(4))
        return ((yh ^ j) * 4 + (x ^ k)) * O_BLK + t

    occ_both = select_cols(occ_coef, jnp.concatenate([occ_source((0, 3, 1, 2)), occ_source((0, 1, 3, 2))]))
    kinds = ((occ_both[:, :96], 1, 3), (occ_both[:, 96:], 3, 1))

    apos = jnp.arange(4 * A_BLK, dtype=jnp.int32)
    a_source = ((yl ^ ((apos // A_BLK) % 2)) * 2 + (core ^ (apos // (2 * A_BLK)))) * A_BLK + apos % A_BLK
    virt = []
    for k in range(4):
        cols = lax.dynamic_slice_in_dim(virt_coef, ((z + k) % 4) * 4 * A_BLK, 4 * A_BLK, axis=1)
        cols = select_cols(cols, a_source)
        virt.append(cols if k == 0 else lax.ppermute(cols, "col", col_z(k)))

    dots = {}
    for kind in (0, 1):
        for ch in CHUNKS:
            lo, hi = ch[kind]
            if (lo, hi, kind) not in dots:
                dots[lo, hi, kind] = jnp.einsum(
                    "mi,mnp->nip", kinds[kind][0], integrals[:, lo:hi], preferred_element_type=F32
                )

    acc = {}
    for ch in CHUNKS:
        p0, p1 = ch[2]
        parts = []
        for kind in (0, 1):
            lo, hi = ch[kind]
            _, first, second = kinds[kind]
            part = dots[lo, hi, kind][:, :, p0:p1]
            recv1 = lax.ppermute(part[:, 48:].astype(BF16), "row", row_perm(first))
            recv2 = lax.ppermute((part[:, 24:48] + recv1[:, 24:]).astype(BF16), "row", row_perm(second))
            parts.append(part[:, :24] + recv1[:, :24] + recv2)
        own = jnp.concatenate(parts, axis=0)
        own = jnp.swapaxes(own, 0, 1)
        recv3 = lax.ppermute(own[O_BLK:].astype(BF16), "row", row_perm(4))
        half = (own[:O_BLK] + recv3).astype(BF16)
        rows = [half] + [lax.ppermute(half, "col", col_z(k)) for k in (1, 2, 3)]
        rows = jnp.concatenate(rows, axis=1)
        cols = jnp.concatenate([v[lo:hi] for v in virt for lo, hi in ch[:2]], axis=0)
        prod = jnp.einsum("inp,na->iap", rows, cols, preferred_element_type=F32)
        acc[p0, p1] = acc[p0, p1] + prod if (p0, p1) in acc else prod

    out = 0.0
    for (p0, p1), total in acc.items():
        recv4 = lax.ppermute(total[:, 2 * A_BLK :].astype(BF16), "col", col_xor(1))
        recv5 = lax.ppermute(
            (total[:, A_BLK : 2 * A_BLK] + recv4[:, A_BLK:]).astype(BF16), "col", col_xor(2)
        )
        slab = (total[:, :A_BLK] + recv4[:, :A_BLK] + recv5).astype(BF16)
        hot = (lax.broadcasted_iota(jnp.int32, (p1 - p0, 256), 0) + p0 == pair_index[None, :]).astype(BF16)
        out = out + jnp.einsum("iap,pk->iak", slab, hot, preferred_element_type=F32)
    return out.astype(BF16)


def solution(mesh):
    return jax.shard_map(
        local,
        mesh=mesh,
        in_specs=(P("row", "col", None), P("row", None), P("col", None), P()),
        out_specs=P("row", "col", None),
        check_vma=False,
    )
```

time: 364 us -> 188 us (0.52)
  waiting for transfers between devices: 282 us -> 75.2 us
  starting transfers between devices: 5.92 us -> 43.2 us
  between operations: 13.5 us -> 0.35 us
  other arithmetic: 3.79 us -> 12.9 us
  matrix products: 26 us -> 21.6 us
    reduce_scatter x1 -> x0, waiting for transfers between devices: 175 us -> none  [local(): lax.psum_scatter(jnp.einsum('mi,mnp->inp', occ_coef, integrals, preferred...]
    all_gather x1 -> x0, waiting for transfers between devices: 78.2 us -> none  [local(): lax.all_gather(half_rows, 'col', axis=1, tiled=True)]
    ppermute x0 -> x21, waiting for transfers between devices: none -> 75.2 us  [the longest x6 21.2 us: local(): rows = [half] + [lax.ppermute(half, 'col', col_z(k)) for k in (1, 2, 3)]]
    ppermute x0 -> x21, starting transfers between devices: none -> 43.2 us  [the longest x4 8.3 us: local(): recv1 = lax.ppermute(part[:, 48:].astype(BF16), 'row', row_perm(first))]
    all_to_all x1 -> x0, waiting for transfers between devices: 29.2 us -> none  [local(): lax.all_to_all(virt_coef, 'col', split_axis=1, concat_axis=0, tiled=True)]
    slice x0 -> x22, local copies, waits for them, and re-layouts: none -> 19.2 us  [the longest x5 11.4 us: local(): integrals[:, lo:hi]]
    dot_general x1 -> x4, local copies, waits for them, and re-layouts: 19 us -> 8.56 us  [local(): jnp.einsum('mi,mnp->nip', kinds[kind][0], integrals[:, lo:hi], preferred_...]
    all_to_all x1 -> x0, starting transfers between devices: 5.88 us -> none  [local(): lax.all_to_all(virt_coef, 'col', split_axis=1, concat_axis=0, tiled=True)]
  transfers between devices with their start and end apart: 3 -> 21, of which waited for: 3 -> 11; matrix products, arithmetic and copies ran while one was open for 1% -> 21% of each run, Pallas kernels for 0% -> 0%
where the time goes in v1:
time: 188 us; the launch traced here: 187 us
  waiting for transfers between devices  75.2 us (40%)
  starting transfers between devices  43.2 us (23%)
  local copies, waits for them, and re-layouts  33.2 us (18%)
  matrix products  21.6 us (11%)
  other arithmetic  12.9 us (7%)
    ppermute x6, waiting for transfers between devices, local(): rows = [half] + [lax.ppermute(half, 'col', col_z(k)) for k in (1, 2, 3)]  21.2 us
    ppermute x1, waiting for transfers between devices, local(): lax.ppermute((total[:, A_BLK:2 * A_BLK] + recv4[:, A_BLK:]).astype(BF16),...  20.4 us
    ppermute x4, waiting for transfers between devices, local(): recv1 = lax.ppermute(part[:, 48:].astype(BF16), 'row', row_perm(first))  18.9 us
    slice x5, local copies, waits for them, and re-layouts, local(): integrals[:, lo:hi]  11.4 us
    dot_general x4, matrix products, local(): jnp.einsum('mi,mnp->nip', kinds[kind][0], integrals[:, lo:hi], preferred_...  10.7 us
    ppermute x4, waiting for transfers between devices, local(): lax.ppermute((part[:, 24:48] + recv1[:, 24:]).astype(BF16), 'row', row_pe...  8.72 us
    dot_general x4, local copies, waits for them, and re-layouts, local(): jnp.einsum('mi,mnp->nip', kinds[kind][0], integrals[:, lo:hi], preferred_...  8.56 us
    ppermute x4, starting transfers between devices, local(): recv1 = lax.ppermute(part[:, 48:].astype(BF16), 'row', row_perm(first))  8.3 us
  transfers between devices with their start and end apart: 21, of which 11 were waited for; matrix products, arithmetic and copies ran while one was open for 21% of the time, Pallas kernels for 0%

profile of v1, /device:TPU:1, one launch (start us, length us, event | category | flops | bytes accessed | tf_op | source)
XLA Modules:
  0.0 186.5 jit_solution(3815396282887914608)
XLA Ops:
  0.0 10.2 %fusion.100 = (bf16[300,40,256]{2,1,0:T(8,128)(2,1)}, bf16[300,40,256]{2,1,0:T(8,128)(2,1)}) fusion(bf16[300,150,256]{2,1,0:T(8,128)(2,1)} %param.4), kind=kLoop, calls=%fused_computation.162 | loop fusion | bytes 24576000 | tf_op jit(solution)/shard_map/slice | solution.py:62
  10.5 4.4 %fusion.2 = f32[96,40,256]{2,0,1:T(8,128)S(1)} fusion(bf16[300,40,256]{2,1,0:T(8,128)(2,1)} %get-tuple-element.5, bf16[300,192]{0,1:T(8,128)(2,1)S(1)} %fusion.34), kind=kOutput, calls=%fused_computation.3 | convolution fusion | flops 589824000 | bytes 10149888 | tf_op jit(solution)/shard_map/mi,mnp->nip/dot_general | solution.py:61
  14.9 2.3 %copy.74 = f32[96,40,256]{2,1,0:T(8,128)S(1)} copy(f32[96,40,256]{2,0,1:T(8,128)S(1)} %fusion.2) | data formatting | bytes 7864320 | tf_op jit(solution)/shard_map/mi,mnp->nip/dot_general | solution.py:61
  17.2 2.0 %copy-done.1 = f32[96,40,256]{2,1,0:T(8,128)} copy-done((f32[96,40,256]{2,1,0:T(8,128)}, f32[96,40,256]{2,1,0:T(8,128)S(1)}, u32[]{:S(2)}) %copy-start.1) | copy-done | bytes 3932184
  19.3 2.1 %collective-permute-start.3 = (bf16[40,48,256]{2,0,1:T(8,128)(2,1)S(1)}, bf16[40,48,256]{2,0,1:T(8,128)(2,1)}, u32[]{:S(2)}, u32[]{:S(2)}) collective-permute-start(bf16[40,48,256]{2,0,1:T(8,128)(2,1)S(1)} %slice.300), channel_id=1, source_target_pairs={{0,16},{16,0},{32,48},{48,32},{64,80},{80,64},{96,112},{112,96},{1... | collective-permute-start | bytes 2949128 | tf_op jit(solution)/shard_map/ppermute | solution.py:73
  21.8 3.2 %fusion.6 = f32[96,32,256]{2,0,1:T(8,128)S(1)} fusion(bf16[300,32,256]{2,1,0:T(8,128)(2,1)S(1)} %slice-done.2, bf16[300,192]{0,1:T(8,128)(2,1)S(1)} %fusion.34), kind=kOutput, calls=%fused_computation.7 | convolution fusion | flops 471859200 | bytes 8134656 | tf_op jit(solution)/shard_map/mi,mnp->nip/dot_general | solution.py:61
  29.5 2.0 %collective-permute-start.11 = (bf16[32,48,256]{2,0,1:T(8,128)(2,1)}, bf16[32,48,256]{2,0,1:T(8,128)(2,1)S(1)}, u32[]{:S(2)}, u32[]{:S(2)}) collective-permute-start(bf16[32,48,256]{2,0,1:T(8,128)(2,1)} %slice.301), channel_id=1, source_target_pairs={{0,16},{16,0},{32,48},{48,32},{64,80},{80,64},{96,112},{112,96},{1... | collective-permute-start | bytes 2359304 | tf_op jit(solution)/shard_map/ppermute | solution.py:73
  33.9 2.2 %copy.72 = f32[96,38,256]{2,1,0:T(8,128)S(1)} copy(f32[96,38,256]{2,0,1:T(8,128)S(1)} %fusion.4) | data formatting | bytes 7471104 | tf_op jit(solution)/shard_map/mi,mnp->nip/dot_general | solution.py:61
  37.5 3.3 %collective-permute-start.13 = (bf16[38,48,256]{2,1,0:T(8,128)(2,1)}, bf16[38,48,256]{2,1,0:T(8,128)(2,1)}, u32[]{:S(2)}, u32[]{:S(2)}) collective-permute-start(bf16[38,48,256]{2,1,0:T(8,128)(2,1)} %copy.49), channel_id=1, source_target_pairs={{0,48},{16,32},{32,16},{48,0},{64,112},{80,96},{96,80},{112,64},{1... | collective-permute-start | bytes 2801672 | tf_op jit(solution)/shard_map/ppermute | solution.py:73
  42.4 2.3 %copy.73 = f32[96,40,256]{2,1,0:T(8,128)S(1)} copy(f32[96,40,256]{2,0,1:T(8,128)S(1)} %fusion) | data formatting | bytes 7864320 | tf_op jit(solution)/shard_map/mi,mnp->nip/dot_general | solution.py:61
  44.7 1.9 copy-done.3
  51.6 7.8 %collective-permute-done.11 = bf16[32,48,256]{2,0,1:T(8,128)(2,1)S(1)} collective-permute-done((bf16[32,48,256]{2,0,1:T(8,128)(2,1)}, bf16[32,48,256]{2,0,1:T(8,128)(2,1)S(1)}, u32[]{:S(2)}, u32[]{:S(2)}) %collective-permute-start.11) | collective-permute-done | bytes 786464 | tf_op jit(solution)/shard_map/ppermute | solution.py:73
  59.4 4.0 %collective-permute-start.1 = (bf16[150,576]{1,0:T(8,128)(2,1)}, bf16[150,576]{1,0:T(8,128)(2,1)}, u32[]{:S(2)}, u32[]{:S(2)}) collective-permute-start(bf16[150,576]{1,0:T(8,128)(2,1)} %fusion.32), channel_id=1, source_target_pairs={{0,8},{1,9},{2,10},{3,11},{4,12},{5,13},{6,14},{7,15},{8,0},{9,1},... | collective-permute-start | bytes 518408 | tf_op jit(solution)/shard_map/ppermute | solution.py:54
  64.7 2.6 %collective-permute-start.12 = (bf16[32,24,256]{2,0,1:T(8,128)(2,1)S(1)}, bf16[32,24,256]{2,0,1:T(8,128)(2,1)S(1)}, u32[]{:S(2)}, u32[]{:S(2)}) collective-permute-start(bf16[32,24,256]{2,0,1:T(8,128)(2,1)S(1)} %fusion.45), channel_id=1, source_target_pairs={{0,48},{16,32},{32,16},{48,0},{64,112},{80,96},{96,80},{112,64},{1... | collective-permute-start | bytes 1179656 | tf_op jit(solution)/shard_map/ppermute | solution.py:74
  71.1 11.1 %collective-permute-done.5 = bf16[40,48,256]{2,0,1:T(8,128)(2,1)} collective-permute-done((bf16[40,48,256]{2,0,1:T(8,128)(2,1)S(1)}, bf16[40,48,256]{2,0,1:T(8,128)(2,1)}, u32[]{:S(2)}, u32[]{:S(2)}) %collective-permute-start.5) | collective-permute-done | bytes 983072 | tf_op jit(solution)/shard_map/ppermute | solution.py:73
  82.2 2.8 %collective-permute-start.4 = (bf16[40,24,256]{2,0,1:T(8,128)(2,1)S(1)}, bf16[40,24,256]{2,0,1:T(8,128)(2,1)S(1)}, u32[]{:S(2)}, u32[]{:S(2)}) collective-permute-start(bf16[40,24,256]{2,0,1:T(8,128)(2,1)S(1)} %fusion.40), channel_id=1, source_target_pairs={{0,48},{16,32},{32,16},{48,0},{64,112},{80,96},{96,80},{112,64},{1... | collective-permute-start | bytes 1474568 | tf_op jit(solution)/shard_map/ppermute | solution.py:74
  86.1 4.4 %collective-permute-done.12 = bf16[32,24,256]{2,0,1:T(8,128)(2,1)S(1)} collective-permute-done((bf16[32,24,256]{2,0,1:T(8,128)(2,1)S(1)}, bf16[32,24,256]{2,0,1:T(8,128)(2,1)S(1)}, u32[]{:S(2)}, u32[]{:S(2)}) %collective-permute-start.12) | collective-permute-done | bytes 393248 | tf_op jit(solution)/shard_map/ppermute | solution.py:74
  93.7 2.9 %collective-permute-start.15 = (bf16[12,70,256]{2,1,0:T(8,128)(2,1)S(1)}, bf16[12,70,256]{2,1,0:T(8,128)(2,1)S(1)}, u32[]{:S(2)}, u32[]{:S(2)}) collective-permute-start(bf16[12,70,256]{2,1,0:T(8,128)(2,1)S(1)} %slice.303), channel_id=1, source_target_pairs={{0,64},{16,80},{32,96},{48,112},{64,0},{80,16},{96,32},{112,48},{1... | collective-permute-start | bytes 1290248 | tf_op jit(solution)/shard_map/ppermute | solution.py:78
  96.7 4.3 %collective-permute-done.4 = bf16[40,24,256]{2,0,1:T(8,128)(2,1)S(1)} collective-permute-done((bf16[40,24,256]{2,0,1:T(8,128)(2,1)S(1)}, bf16[40,24,256]{2,0,1:T(8,128)(2,1)S(1)}, u32[]{:S(2)}, u32[]{:S(2)}) %collective-permute-start.4) | collective-permute-done | bytes 491552 | tf_op jit(solution)/shard_map/ppermute | solution.py:74
  103.7 3.3 %collective-permute-start.7 = (bf16[12,80,256]{2,1,0:T(8,128)(2,1)S(1)}, bf16[12,80,256]{2,1,0:T(8,128)(2,1)}, u32[]{:S(2)}, u32[]{:S(2)}) collective-permute-start(bf16[12,80,256]{2,1,0:T(8,128)(2,1)S(1)} %slice.302), channel_id=1, source_target_pairs={{0,64},{16,80},{32,96},{48,112},{64,0},{80,16},{96,32},{112,48},{1... | collective-permute-start | bytes 1474568 | tf_op jit(solution)/shard_map/ppermute | solution.py:78
  110.7 2.1 %collective-permute-start.2 = (bf16[150,576]{1,0:T(8,128)(2,1)}, bf16[150,576]{1,0:T(8,128)(2,1)S(1)}, u32[]{:S(2)}, u32[]{:S(2)}) collective-permute-start(bf16[150,576]{1,0:T(8,128)(2,1)} %fusion.33), channel_id=1, source_target_pairs={{0,12},{1,13},{2,14},{3,15},{4,0},{5,1},{6,2},{7,3},{8,4},{9,5},{1... | collective-permute-start | bytes 518408 | tf_op jit(solution)/shard_map/ppermute | solution.py:54
  114.2 2.7 %collective-permute-done.7 = bf16[12,80,256]{2,1,0:T(8,128)(2,1)} collective-permute-done((bf16[12,80,256]{2,1,0:T(8,128)(2,1)S(1)}, bf16[12,80,256]{2,1,0:T(8,128)(2,1)}, u32[]{:S(2)}, u32[]{:S(2)}) %collective-permute-start.7) | collective-permute-done | bytes 491552 | tf_op jit(solution)/shard_map/ppermute | solution.py:78
  116.8 3.6 %collective-permute-start.18 = (bf16[12,70,256]{2,1,0:T(8,128)(2,1)}, bf16[12,70,256]{2,1,0:T(8,128)(2,1)S(1)}, u32[]{:S(2)}, u32[]{:S(2)}) collective-permute-start(bf16[12,70,256]{2,1,0:T(8,128)(2,1)} %fusion.44), channel_id=1, source_target_pairs={{0,12},{1,13},{2,14},{3,15},{4,0},{5,1},{6,2},{7,3},{8,4},{9,5},{1... | collective-permute-start | bytes 1290248 | tf_op jit(solution)/shard_map/ppermute | solution.py:80
  127.3 3.4 %collective-permute-done.17 = bf16[12,70,256]{2,1,0:T(8,128)(2,1)S(1)} collective-permute-done((bf16[12,70,256]{2,1,0:T(8,128)(2,1)}, bf16[12,70,256]{2,1,0:T(8,128)(2,1)S(1)}, u32[]{:S(2)}, u32[]{:S(2)}) %collective-permute-start.17) | collective-permute-done | bytes 430112 | tf_op jit(solution)/shard_map/ppermute | solution.py:80
  130.7 5.8 %collective-permute-done.18 = bf16[12,70,256]{2,1,0:T(8,128)(2,1)S(1)} collective-permute-done((bf16[12,70,256]{2,1,0:T(8,128)(2,1)}, bf16[12,70,256]{2,1,0:T(8,128)(2,1)S(1)}, u32[]{:S(2)}, u32[]{:S(2)}) %collective-permute-start.18) | collective-permute-done | bytes 430112 | tf_op jit(solution)/shard_map/ppermute | solution.py:80
  136.5 3.2 %fusion.18 = f32[576,12,256]{2,0,1:T(8,128)S(1)} fusion(bf16[12,70,256]{2,1,0:T(8,128)(2,1)S(1)} %collective-permute-done.18, bf16[12,70,256]{2,1,0:T(8,128)(2,1)S(1)} %collective-permute-done.17, bf16[12,70,256]{2,1,0:T(8,128)(2,1)} %collective-permute-done.16, bf16[12,70,256]{2,1,0:T(8,128)(2,1)} %fusion.44, bf16[70,576]{1,0:T(8,128)(2,1)S(1)} %slice.216, ...), kind=kOutput, calls=%fused_computation.31 | convolution fusion | flops 999075840 | bytes 9120768 | tf_op jit(solution)/shard_map/inp,na->iap/dot_general | solution.py:83
  139.7 9.0 %collective-permute-done.10 = bf16[12,80,256]{2,1,0:T(8,128)(2,1)S(1)} collective-permute-done((bf16[12,80,256]{2,1,0:T(8,128)(2,1)S(1)}, bf16[12,80,256]{2,1,0:T(8,128)(2,1)S(1)}, u32[]{:S(2)}, u32[]{:S(2)}) %collective-permute-start.10) | collective-permute-done | bytes 491552 | tf_op jit(solution)/shard_map/ppermute | solution.py:80
  148.7 3.1 %collective-permute-done.9 = bf16[12,80,256]{2,1,0:T(8,128)(2,1)S(1)} collective-permute-done((bf16[12,80,256]{2,1,0:T(8,128)(2,1)S(1)}, bf16[12,80,256]{2,1,0:T(8,128)(2,1)S(1)}, u32[]{:S(2)}, u32[]{:S(2)}) %collective-permute-start.9) | collective-permute-done | bytes 491552 | tf_op jit(solution)/shard_map/ppermute | solution.py:80
  151.8 2.0 %add_bitcast_fusion = f32[12,576,256]{2,1,0:T(8,128)S(1)} fusion(f32[576,12,256]{2,0,1:T(8,128)S(1)} %fusion.18, bf16[12,80,256]{2,1,0:T(8,128)(2,1)S(1)} %collective-permute-done.10, bf16[12,80,256]{2,1,0:T(8,128)(2,1)S(1)} %collective-permute-done.9, bf16[12,80,256]{2,1,0:T(8,128)(2,1)S(1)} %collective-permute-done.8, bf16[12,80,256]{2,1,0:T(8,128)(2,1)S(1)} %fusion.37, ...), kind=kOutput, calls=%fused_computation | convolution fusion | flops 1143570432 | bytes 16490496 | tf_op jit(solution)/shard_map/inp,na->iap/dot_general | solution.py:83
  154.0 6.5 %collective-permute-start.19 = (bf16[12,288,256]{2,1,0:T(8,128)(2,1)S(1)}, bf16[12,288,256]{2,1,0:T(8,128)(2,1)S(1)}, u32[]{:S(2)}, u32[]{:S(2)}) collective-permute-start(bf16[12,288,256]{2,1,0:T(8,128)(2,1)S(1)} %slice.297), channel_id=1, source_target_pairs={{0,1},{1,0},{2,3},{3,2},{4,5},{5,4},{6,7},{7,6},{8,9},{9,8},{10,11... | collective-permute-start | bytes 5308424 | tf_op jit(solution)/shard_map/ppermute | solution.py:88
  160.6 3.3 %collective-permute-done.19 = bf16[12,288,256]{2,1,0:T(8,128)(2,1)S(1)} collective-permute-done((bf16[12,288,256]{2,1,0:T(8,128)(2,1)S(1)}, bf16[12,288,256]{2,1,0:T(8,128)(2,1)S(1)}, u32[]{:S(2)}, u32[]{:S(2)}) %collective-permute-start.19) | collective-permute-done | bytes 1769504 | tf_op jit(solution)/shard_map/ppermute | solution.py:88
  164.7 20.4 %collective-permute-done.20 = bf16[12,144,256]{2,1,0:T(8,128)(2,1)S(1)} collective-permute-done((bf16[12,144,256]{2,1,0:T(8,128)(2,1)S(1)}, bf16[12,144,256]{2,1,0:T(8,128)(2,1)S(1)}, u32[]{:S(2)}, u32[]{:S(2)}) %collective-permute-start.20) | collective-permute-done | bytes 884768 | tf_op jit(solution)/shard_map/ppermute | solution.py:89
  (87 shorter events, 42.2 us)
Async XLA Ops:
  0.0 47.5 %copy-start = (bf16[150,2304]{1,0:T(8,128)(2,1)S(1)}, bf16[150,2304]{1,0:T(8,128)(2,1)}, u32[]{:S(2)}) copy-start(bf16[150,2304]{1,0:T(8,128)(2,1)} %param.6) | copy-start | bytes 2073604
  0.0 10.3 %copy-start.7 = (bf16[300,96]{0,1:T(8,128)(2,1)S(1)}, bf16[300,96]{0,1:T(8,128)(2,1)}, u32[]{:S(2)}) copy-start(bf16[300,96]{0,1:T(8,128)(2,1)} %param.5) | copy-start | bytes 172804
  17.2 2.0 %copy-start.1 = (f32[96,40,256]{2,1,0:T(8,128)}, f32[96,40,256]{2,1,0:T(8,128)S(1)}, u32[]{:S(2)}) copy-start(f32[96,40,256]{2,1,0:T(8,128)S(1)} %copy.74) | copy-start | bytes 11796484
  19.3 2.5 %slice-start.2 = ((bf16[300,150,256]{2,1,0:T(8,128)(2,1)}), bf16[300,32,256]{2,1,0:T(8,128)(2,1)S(1)}, s32[]{:S(2)}) async-start(bf16[300,150,256]{2,1,0:T(8,128)(2,1)} %param.4), calls=%async_computation.2 | async-start | bytes 9830400 | tf_op jit(solution)/shard_map/slice | solution.py:62
  19.3 50.5 %collective-permute-start.3 = (bf16[40,48,256]{2,0,1:T(8,128)(2,1)S(1)}, bf16[40,48,256]{2,0,1:T(8,128)(2,1)}, u32[]{:S(2)}, u32[]{:S(2)}) collective-permute-start(bf16[40,48,256]{2,0,1:T(8,128)(2,1)S(1)} %slice.300), channel_id=1, source_target_pairs={{0,16},{16,0},{32,48},{48,32},{64,80},{80,64},{96,112},{112,96},{1... | collective-permute-start | bytes 2949128 | tf_op jit(solution)/shard_map/ppermute | solution.py:73
  29.5 2.8 %slice-start.3 = ((bf16[300,150,256]{2,1,0:T(8,128)(2,1)}), bf16[300,38,256]{2,1,0:T(8,128)(2,1)S(1)}, s32[]{:S(2)}) async-start(bf16[300,150,256]{2,1,0:T(8,128)(2,1)} %param.4), calls=%async_computation.3 | async-start | bytes 12288000 | tf_op jit(solution)/shard_map/slice | solution.py:62
  29.5 29.9 %collective-permute-start.11 = (bf16[32,48,256]{2,0,1:T(8,128)(2,1)}, bf16[32,48,256]{2,0,1:T(8,128)(2,1)S(1)}, u32[]{:S(2)}, u32[]{:S(2)}) collective-permute-start(bf16[32,48,256]{2,0,1:T(8,128)(2,1)} %slice.301), channel_id=1, source_target_pairs={{0,16},{16,0},{32,48},{48,32},{64,80},{80,64},{96,112},{112,96},{1... | collective-permute-start | bytes 2359304 | tf_op jit(solution)/shard_map/ppermute | solution.py:73
  32.3 8.5 %slice-start = ((s8[6144000]{0:T(1024)(128)(4,1)}), s8[4194304]{0:T(1024)(128)(4,1)S(1)}, s32[]{:S(2)}) async-start(s8[6144000]{0:T(1024)(128)(4,1)} %bitcast.38), calls=%async_computation | async-start | bytes 8388608
  33.9 6.9 %slice-start.1 = ((s8[6144000]{0:T(1024)(128)(4,1)}), s8[1949696]{0:T(1024)(128)(4,1)S(1)}, s32[]{:S(2)}) async-start(s8[6144000]{0:T(1024)(128)(4,1)} %bitcast.38), calls=%async_computation.1 | async-start | bytes 3899392
  36.0 4.7 %copy-start.5 = (f32[96,38,256]{2,1,0:T(8,128)}, f32[96,38,256]{2,1,0:T(8,128)S(1)}, u32[]{:S(2)}) copy-start(f32[96,38,256]{2,1,0:T(8,128)S(1)} %copy.72) | copy-start | bytes 11206660
  37.5 27.1 %collective-permute-start.13 = (bf16[38,48,256]{2,1,0:T(8,128)(2,1)}, bf16[38,48,256]{2,1,0:T(8,128)(2,1)}, u32[]{:S(2)}, u32[]{:S(2)}) collective-permute-start(bf16[38,48,256]{2,1,0:T(8,128)(2,1)} %copy.49), channel_id=1, source_target_pairs={{0,48},{16,32},{32,16},{48,0},{64,112},{80,96},{96,80},{112,64},{1... | collective-permute-start | bytes 2801672 | tf_op jit(solution)/shard_map/ppermute | solution.py:73
  46.6 35.5 %collective-permute-start.5 = (bf16[40,48,256]{2,0,1:T(8,128)(2,1)S(1)}, bf16[40,48,256]{2,0,1:T(8,128)(2,1)}, u32[]{:S(2)}, u32[]{:S(2)}) collective-permute-start(bf16[40,48,256]{2,0,1:T(8,128)(2,1)S(1)} %slice.299), channel_id=1, source_target_pairs={{0,48},{16,32},{32,16},{48,0},{64,112},{80,96},{96,80},{112,64},{1... | collective-permute-start | bytes 2949128 | tf_op jit(solution)/shard_map/ppermute | solution.py:73
  48.7 64.2 %collective-permute-start = (bf16[150,576]{1,0:T(8,128)(2,1)}, bf16[150,576]{1,0:T(8,128)(2,1)}, u32[]{:S(2)}, u32[]{:S(2)}) collective-permute-start(bf16[150,576]{1,0:T(8,128)(2,1)} %fusion.31), channel_id=1, source_target_pairs={{0,4},{1,5},{2,6},{3,7},{4,8},{5,9},{6,10},{7,11},{8,12},{9,13},{1... | collective-permute-start | bytes 518408 | tf_op jit(solution)/shard_map/ppermute | solution.py:54
  50.4 19.5 %copy-start.2 = (f32[96,40,256]{2,1,0:T(8,128)S(1)}, f32[96,40,256]{2,1,0:T(8,128)}, u32[]{:S(2)}) copy-start(f32[96,40,256]{2,1,0:T(8,128)} %copy-done.1) | copy-start | bytes 11796484
  51.6 33.3 %copy-start.4 = (f32[96,40,256]{2,1,0:T(8,128)S(1)}, f32[96,40,256]{2,1,0:T(8,128)}, u32[]{:S(2)}) copy-start(f32[96,40,256]{2,1,0:T(8,128)} %copy-done.3) | copy-start | bytes 11796484
  59.4 62.2 %collective-permute-start.1 = (bf16[150,576]{1,0:T(8,128)(2,1)}, bf16[150,576]{1,0:T(8,128)(2,1)}, u32[]{:S(2)}, u32[]{:S(2)}) collective-permute-start(bf16[150,576]{1,0:T(8,128)(2,1)} %fusion.32), channel_id=1, source_target_pairs={{0,8},{1,9},{2,10},{3,11},{4,12},{5,13},{6,14},{7,15},{8,0},{9,1},... | collective-permute-start | bytes 518408 | tf_op jit(solution)/shard_map/ppermute | solution.py:54
  64.7 25.8 %collective-permute-start.12 = (bf16[32,24,256]{2,0,1:T(8,128)(2,1)S(1)}, bf16[32,24,256]{2,0,1:T(8,128)(2,1)S(1)}, u32[]{:S(2)}, u32[]{:S(2)}) collective-permute-start(bf16[32,24,256]{2,0,1:T(8,128)(2,1)S(1)} %fusion.45), channel_id=1, source_target_pairs={{0,48},{16,32},{32,16},{48,0},{64,112},{80,96},{96,80},{112,64},{1... | collective-permute-start | bytes 1179656 | tf_op jit(solution)/shard_map/ppermute | solution.py:74
  69.8 22.3 %collective-permute-start.14 = (bf16[38,24,256]{2,0,1:T(8,128)(2,1)S(1)}, bf16[38,24,256]{2,0,1:T(8,128)(2,1)S(1)}, u32[]{:S(2)}, u32[]{:S(2)}) collective-permute-start(bf16[38,24,256]{2,0,1:T(8,128)(2,1)S(1)} %fusion.35), channel_id=1, source_target_pairs={{0,16},{16,0},{32,48},{48,32},{64,80},{80,64},{96,112},{112,96},{1... | collective-permute-start | bytes 1400840 | tf_op jit(solution)/shard_map/ppermute | solution.py:74
  82.2 18.9 %collective-permute-start.4 = (bf16[40,24,256]{2,0,1:T(8,128)(2,1)S(1)}, bf16[40,24,256]{2,0,1:T(8,128)(2,1)S(1)}, u32[]{:S(2)}, u32[]{:S(2)}) collective-permute-start(bf16[40,24,256]{2,0,1:T(8,128)(2,1)S(1)} %fusion.40), channel_id=1, source_target_pairs={{0,48},{16,32},{32,16},{48,0},{64,112},{80,96},{96,80},{112,64},{1... | collective-permute-start | bytes 1474568 | tf_op jit(solution)/shard_map/ppermute | solution.py:74
  90.5 11.7 %collective-permute-start.6 = (bf16[40,24,256]{2,0,1:T(8,128)(2,1)S(1)}, bf16[40,24,256]{2,0,1:T(8,128)(2,1)S(1)}, u32[]{:S(2)}, u32[]{:S(2)}) collective-permute-start(bf16[40,24,256]{2,0,1:T(8,128)(2,1)S(1)} %fusion.38), channel_id=1, source_target_pairs={{0,16},{16,0},{32,48},{48,32},{64,80},{80,64},{96,112},{112,96},{1... | collective-permute-start | bytes 1474568 | tf_op jit(solution)/shard_map/ppermute | solution.py:74
  93.7 13.3 %collective-permute-start.15 = (bf16[12,70,256]{2,1,0:T(8,128)(2,1)S(1)}, bf16[12,70,256]{2,1,0:T(8,128)(2,1)S(1)}, u32[]{:S(2)}, u32[]{:S(2)}) collective-permute-start(bf16[12,70,256]{2,1,0:T(8,128)(2,1)S(1)} %slice.303), channel_id=1, source_target_pairs={{0,64},{16,80},{32,96},{48,112},{64,0},{80,16},{96,32},{112,48},{1... | collective-permute-start | bytes 1290248 | tf_op jit(solution)/shard_map/ppermute | solution.py:78
  103.7 13.1 %collective-permute-start.7 = (bf16[12,80,256]{2,1,0:T(8,128)(2,1)S(1)}, bf16[12,80,256]{2,1,0:T(8,128)(2,1)}, u32[]{:S(2)}, u32[]{:S(2)}) collective-permute-start(bf16[12,80,256]{2,1,0:T(8,128)(2,1)S(1)} %slice.302), channel_id=1, source_target_pairs={{0,64},{16,80},{32,96},{48,112},{64,0},{80,16},{96,32},{112,48},{1... | collective-permute-start | bytes 1474568 | tf_op jit(solution)/shard_map/ppermute | solution.py:78
  107.9 15.2 %collective-permute-start.16 = (bf16[12,70,256]{2,1,0:T(8,128)(2,1)}, bf16[12,70,256]{2,1,0:T(8,128)(2,1)}, u32[]{:S(2)}, u32[]{:S(2)}) collective-permute-start(bf16[12,70,256]{2,1,0:T(8,128)(2,1)} %fusion.44), channel_id=1, source_target_pairs={{0,4},{1,5},{2,6},{3,7},{4,8},{5,9},{6,10},{7,11},{8,12},{9,13},{1... | collective-permute-start | bytes 1290248 | tf_op jit(solution)/shard_map/ppermute | solution.py:80
  110.7 11.0 %collective-permute-start.2 = (bf16[150,576]{1,0:T(8,128)(2,1)}, bf16[150,576]{1,0:T(8,128)(2,1)S(1)}, u32[]{:S(2)}, u32[]{:S(2)}) collective-permute-start(bf16[150,576]{1,0:T(8,128)(2,1)} %fusion.33), channel_id=1, source_target_pairs={{0,12},{1,13},{2,14},{3,15},{4,0},{5,1},{6,2},{7,3},{8,4},{9,5},{1... | collective-permute-start | bytes 518408 | tf_op jit(solution)/shard_map/ppermute | solution.py:54
  112.9 17.8 %collective-permute-start.17 = (bf16[12,70,256]{2,1,0:T(8,128)(2,1)}, bf16[12,70,256]{2,1,0:T(8,128)(2,1)S(1)}, u32[]{:S(2)}, u32[]{:S(2)}) collective-permute-start(bf16[12,70,256]{2,1,0:T(8,128)(2,1)} %fusion.44), channel_id=1, source_target_pairs={{0,8},{1,9},{2,10},{3,11},{4,12},{5,13},{6,14},{7,15},{8,0},{9,1},... | collective-permute-start | bytes 1290248 | tf_op jit(solution)/shard_map/ppermute | solution.py:80
  116.8 19.7 %collective-permute-start.18 = (bf16[12,70,256]{2,1,0:T(8,128)(2,1)}, bf16[12,70,256]{2,1,0:T(8,128)(2,1)S(1)}, u32[]{:S(2)}, u32[]{:S(2)}) collective-permute-start(bf16[12,70,256]{2,1,0:T(8,128)(2,1)} %fusion.44), channel_id=1, source_target_pairs={{0,12},{1,13},{2,14},{3,15},{4,0},{5,1},{6,2},{7,3},{8,4},{9,5},{1... | collective-permute-start | bytes 1290248 | tf_op jit(solution)/shard_map/ppermute | solution.py:80
  121.6 27.1 %collective-permute-start.10 = (bf16[12,80,256]{2,1,0:T(8,128)(2,1)S(1)}, bf16[12,80,256]{2,1,0:T(8,128)(2,1)S(1)}, u32[]{:S(2)}, u32[]{:S(2)}) collective-permute-start(bf16[12,80,256]{2,1,0:T(8,128)(2,1)S(1)} %fusion.37), channel_id=1, source_target_pairs={{0,12},{1,13},{2,14},{3,15},{4,0},{5,1},{6,2},{7,3},{8,4},{9,5},{1... | collective-permute-start | bytes 1474568 | tf_op jit(solution)/shard_map/ppermute | solution.py:80
  121.8 26.9 %collective-permute-start.8 = (bf16[12,80,256]{2,1,0:T(8,128)(2,1)S(1)}, bf16[12,80,256]{2,1,0:T(8,128)(2,1)S(1)}, u32[]{:S(2)}, u32[]{:S(2)}) collective-permute-start(bf16[12,80,256]{2,1,0:T(8,128)(2,1)S(1)} %fusion.37), channel_id=1, source_target_pairs={{0,4},{1,5},{2,6},{3,7},{4,8},{5,9},{6,10},{7,11},{8,12},{9,13},{1... | collective-permute-start | bytes 1474568 | tf_op jit(solution)/shard_map/ppermute | solution.py:80
  123.1 28.6 %collective-permute-start.9 = (bf16[12,80,256]{2,1,0:T(8,128)(2,1)S(1)}, bf16[12,80,256]{2,1,0:T(8,128)(2,1)S(1)}, u32[]{:S(2)}, u32[]{:S(2)}) collective-permute-start(bf16[12,80,256]{2,1,0:T(8,128)(2,1)S(1)} %fusion.37), channel_id=1, source_target_pairs={{0,8},{1,9},{2,10},{3,11},{4,12},{5,13},{6,14},{7,15},{8,0},{9,1},... | collective-permute-start | bytes 1474568 | tf_op jit(solution)/shard_map/ppermute | solution.py:80
  153.8 31.3 %copy-start.8 = (s32[256]{0:T(256)S(1)}, s32[256]{0:T(256)}, u32[]{:S(2)}) copy-start(s32[256]{0:T(256)} %param.7) | copy-start | bytes 3076
  154.0 9.9 %collective-permute-start.19 = (bf16[12,288,256]{2,1,0:T(8,128)(2,1)S(1)}, bf16[12,288,256]{2,1,0:T(8,128)(2,1)S(1)}, u32[]{:S(2)}, u32[]{:S(2)}) collective-permute-start(bf16[12,288,256]{2,1,0:T(8,128)(2,1)S(1)} %slice.297), channel_id=1, source_target_pairs={{0,1},{1,0},{2,3},{3,2},{4,5},{5,4},{6,7},{7,6},{8,9},{9,8},{10,11... | collective-permute-start | bytes 5308424 | tf_op jit(solution)/shard_map/ppermute | solution.py:88
  164.2 20.9 %collective-permute-start.20 = (bf16[12,144,256]{2,1,0:T(8,128)(2,1)S(1)}, bf16[12,144,256]{2,1,0:T(8,128)(2,1)S(1)}, u32[]{:S(2)}, u32[]{:S(2)}) collective-permute-start(bf16[12,144,256]{2,1,0:T(8,128)(2,1)S(1)} %fusion.15), channel_id=1, source_target_pairs={{0,2},{1,3},{2,0},{3,1},{4,6},{5,7},{6,4},{7,5},{8,10},{9,11},{10,... | collective-permute-start | bytes 2654216 | tf_op jit(solution)/shard_map/ppermute | solution.py:89
  (2 other events, 3.5 us)

commit v2 on v0

v2 whole, which is shorter than its diff:
```python
import jax
import jax.numpy as jnp
from jax import lax
from jax.experimental.layout import Layout, with_layout_constraint
from jax.sharding import PartitionSpec as P


F32, BF16 = jnp.float32, jnp.bfloat16
B = 12
A_BLK = 144
H = 128
CHUNKS = {"p": ("x", 0, 40), "q": ("y", 40, 88), "r": ("x", 88, 120, 150)}


def row_perm(mask):
    return [(i, i ^ mask) for i in range(8)]


def col_xor(mask):
    return [(i, i ^ mask) for i in range(16)]


def col_z(k):
    return [(i, (i + 4 * k) % 16) for i in range(16)]


def rowmajor(v):
    return with_layout_constraint(v, Layout(major_to_minor=tuple(range(v.ndim))))


def row(v, mask):
    return lax.ppermute(v, "row", row_perm(mask))


def select_cols(mat, source):
    hot = (lax.broadcasted_iota(jnp.int32, (mat.shape[1], source.shape[0]), 0) == source[None, :]).astype(BF16)
    return jnp.dot(mat, hot, preferred_element_type=F32).astype(BF16)


def f32(v):
    return v.astype(F32)


def x_first(d):
    a1 = row(d[2 * B : 6 * B, :, :H], 1)
    b1 = row(d[4 * B :, :, H:], 3)
    da, a1 = lax.optimization_barrier((d, a1))
    a2 = row((f32(da[6 * B :, :, :H]) + a1[2 * B :]).astype(BF16), 3)
    db, b1 = lax.optimization_barrier((d, b1))
    b2 = row((f32(db[2 * B : 4 * B, :, H:]) + b1[: 2 * B]).astype(BF16), 1)
    d, a2, b2 = lax.optimization_barrier((d, a2, b2))
    own = jnp.concatenate(
        [f32(d[: 2 * B, :, :H]) + a1[: 2 * B] + a2, f32(d[: 2 * B, :, H:]) + b1[2 * B :] + b2], axis=2
    )
    y = row(own[B:].astype(BF16), 4)
    return (own[:B] + y).astype(BF16)


def y_first(d, cols):
    y = row(d[4 * B :], 4)
    s = f32(d[: 4 * B]) + y
    a1 = row(s[B : 3 * B, :, :H].astype(BF16), 1)
    b1 = row(s[2 * B :, :, H:].astype(BF16), 3)
    s, a1, b1, *cols = lax.optimization_barrier((s, a1, b1, *cols))
    a2 = row((s[3 * B :, :, :H] + a1[B:]).astype(BF16), 3)
    b2 = row((s[B : 2 * B, :, H:] + b1[:B]).astype(BF16), 1)
    s, a2, b2 = lax.optimization_barrier((s, a2, b2))
    own = jnp.concatenate([s[:B, :, :H] + a1[:B] + a2, s[:B, :, H:] + b1[B:] + b2], axis=2)
    return own.astype(BF16), *cols


def local(integrals, occ_coef, virt_coef, pair_index):
    r = lax.axis_index("row")
    c = lax.axis_index("col")
    yh, x = r // 4, r % 4
    z, yl, core = c // 4, (c // 2) % 2, c % 2

    pos = jnp.arange(96, dtype=jnp.int32)
    source = {
        "x": ((yh ^ ((pos // B) % 2)) * 4 + (x ^ (pos // (2 * B)))) * B + pos % B,
        "y": ((yh ^ (pos // (4 * B))) * 4 + (x ^ ((pos // B) % 4))) * B + pos % B,
    }
    both = select_cols(occ_coef, jnp.concatenate([source["x"], source["y"]]))
    occ = {"x": both[:, :96], "y": both[:, 96:]}

    products, held = {}, occ_coef
    for name, (kind, *cuts) in CHUNKS.items():
        pieces = []
        for lo, hi in zip(cuts[:-1], cuts[1:]):
            weights = lax.optimization_barrier((occ[kind], held))[0]
            d = jnp.einsum("mi,mnp->inp", weights, integrals[:, lo:hi], preferred_element_type=F32).astype(BF16)
            held = rowmajor(d)
            pieces.append(held)
        products[name] = jnp.concatenate(pieces, axis=1)
    virt_coef = lax.optimization_barrier((virt_coef, held))[0]

    apos = jnp.arange(4 * A_BLK, dtype=jnp.int32)
    a_source = ((yl ^ ((apos // A_BLK) % 2)) * 2 + (core ^ (apos // (2 * A_BLK)))) * A_BLK + apos % A_BLK
    virt = {}
    for k in (0, 1, 3, 2):
        v = lax.dynamic_slice_in_dim(virt_coef, ((z + k) % 4) * 4 * A_BLK, 4 * A_BLK, axis=1)
        v = select_cols(v, a_source)
        virt[k] = v if k == 0 else lax.ppermute(v, "col", col_z(k))

    cols = {}
    for name, (_, *cuts) in CHUNKS.items():
        cols[name] = jnp.concatenate([virt[k][cuts[0] : cuts[-1]] for k in range(4)], axis=0)

    acc = 0.0
    for name, (kind, *_) in sorted(CHUNKS.items(), key=lambda item: item[1][0] == "x"):
        d = products[name]
        if kind == "x":
            half = x_first(d)
        else:
            names = tuple(cols)
            half, *tied = y_first(d, [cols[n] for n in names])
            cols = dict(zip(names, tied))
        h = [half] + [lax.ppermute(half, "col", col_z(k)) for k in (1, 2, 3)]
        acc = acc + jnp.einsum("inp,na->iap", jnp.concatenate(h, axis=1), cols[name], preferred_element_type=F32)

    r4 = lax.ppermute(acc[:, 2 * A_BLK :].astype(BF16), "col", col_xor(1))
    r5 = lax.ppermute((acc[:, A_BLK : 2 * A_BLK] + r4[:, A_BLK:]).astype(BF16), "col", col_xor(2))
    slab = (acc[:, :A_BLK] + r4[:, :A_BLK] + r5).astype(BF16)
    hot = (lax.broadcasted_iota(jnp.int32, (256, 256), 0) == pair_index[None, :]).astype(BF16)
    return jnp.einsum("iap,pk->iak", slab, hot, preferred_element_type=F32).astype(BF16)


def solution(mesh):
    return jax.shard_map(
        local,
        mesh=mesh,
        in_specs=(P("row", "col", None), P("row", None), P("col", None), P()),
        out_specs=P("row", "col", None),
        check_vma=False,
    )
```

time: 364 us -> 177 us (0.49)
  waiting for transfers between devices: 282 us -> 73 us
  starting transfers between devices: 5.92 us -> 48.4 us
  between operations: 13.5 us -> 0.46 us
  local copies, waits for them, and re-layouts: 32.4 us -> 25.6 us
    reduce_scatter x1 -> x0, waiting for transfers between devices: 175 us -> none  [local(): lax.psum_scatter(jnp.einsum('mi,mnp->inp', occ_coef, integrals, preferred...]
    all_gather x1 -> x0, waiting for transfers between devices: 78.2 us -> none  [local(): lax.all_gather(half_rows, 'col', axis=1, tiled=True)]
    ppermute x0 -> x29, waiting for transfers between devices: none -> 73 us  [the longest x15 34 us: row(): return lax.ppermute(v, 'row', row_perm(mask))]
    ppermute x0 -> x29, starting transfers between devices: none -> 48.4 us  [the longest x9 16.4 us: local(): h = [half] + [lax.ppermute(half, 'col', col_z(k)) for k in (1, 2, 3)]]
    all_to_all x1 -> x0, waiting for transfers between devices: 29.2 us -> none  [local(): lax.all_to_all(virt_coef, 'col', split_axis=1, concat_axis=0, tiled=True)]
    slice x0 -> x30, local copies, waits for them, and re-layouts: none -> 16.7 us  [the longest x7 5.9 us: local(): integrals[:, lo:hi]]
    dot_general x1 -> x3, local copies, waits for them, and re-layouts: 19 us -> 4.74 us  [local(): jnp.einsum('mi,mnp->inp', weights, integrals[:, lo:hi], preferred_element...]
    all_to_all x1 -> x0, starting transfers between devices: 5.88 us -> none  [local(): lax.all_to_all(virt_coef, 'col', split_axis=1, concat_axis=0, tiled=True)]
  transfers between devices with their start and end apart: 3 -> 29, of which waited for: 3 -> 12; matrix products, arithmetic and copies ran while one was open for 1% -> 12% of each run, Pallas kernels for 0% -> 0%
where the time goes in v2:
time: 177 us; the launch traced here: 176 us
  waiting for transfers between devices  73 us (41%)
  starting transfers between devices  48.4 us (27%)
  local copies, waits for them, and re-layouts  25.6 us (14%)
  matrix products  22.6 us (13%)
  other arithmetic  6.21 us (4%)
    ppermute x15, waiting for transfers between devices, row(): return lax.ppermute(v, 'row', row_perm(mask))  34 us
    ppermute x1, waiting for transfers between devices, local(): lax.ppermute((acc[:, A_BLK:2 * A_BLK] + r4[:, A_BLK:]).astype(BF16), 'col...  19.5 us
    ppermute x9, starting transfers between devices, local(): h = [half] + [lax.ppermute(half, 'col', col_z(k)) for k in (1, 2, 3)]  16.4 us
    ppermute x9, waiting for transfers between devices, local(): h = [half] + [lax.ppermute(half, 'col', col_z(k)) for k in (1, 2, 3)]  16.1 us
    ppermute x15, starting transfers between devices, row(): return lax.ppermute(v, 'row', row_perm(mask))  15.2 us
    dot_general x4, matrix products, local(): jnp.einsum('mi,mnp->inp', weights, integrals[:, lo:hi], preferred_element...  13.7 us
    ppermute x3, starting transfers between devices, local(): virt[k] = v if k == 0 else lax.ppermute(v, 'col', col_z(k))  8.69 us
    ppermute x1, starting transfers between devices, local(): r4 = lax.ppermute(acc[:, 2 * A_BLK:].astype(BF16), 'col', col_xor(1))  6.83 us
  transfers between devices with their start and end apart: 29, of which 12 were waited for; matrix products, arithmetic and copies ran while one was open for 12% of the time, Pallas kernels for 0%

profile of v2, /device:TPU:1, one launch (start us, length us, event | category | flops | bytes accessed | tf_op | source)
XLA Modules:
  0.0 176.3 jit_solution(15800131621706205608)
XLA Ops:
  0.0 5.9 %slice.184 = bf16[300,40,256]{2,1,0:T(8,128)(2,1)} slice(bf16[300,150,256]{2,1,0:T(8,128)(2,1)} %param.4), slice={[0:300], [0:40], [0:256]} | slice | bytes 12288000 | tf_op jit(solution)/shard_map/slice | solution.py:91
  7.1 4.5 %fusion.2 = bf16[96,40,256]{2,0,1:T(8,128)(2,1)S(1)} fusion(bf16[300,40,256]{2,1,0:T(8,128)(2,1)} %slice.184, bf16[300,96]{0,1:T(8,128)(2,1)S(1)} %get-tuple-element.36), kind=kOutput, calls=%fused_computation.3 | convolution fusion | flops 589824000 | bytes 8167680 | tf_op jit(solution)/shard_map/mi,mnp->inp/dot_general | solution.py:91
  12.7 2.7 %fusion = bf16[96,48,256]{2,0,1:T(8,128)(2,1)S(1)} fusion(bf16[300,48,256]{2,1,0:T(8,128)(2,1)S(1)} %slice-done, bf16[300,96]{0,1:T(8,128)(2,1)S(1)} %get-tuple-element.34), kind=kOutput, calls=%fused_computation | convolution fusion | flops 707788800 | bytes 9789696 | tf_op jit(solution)/shard_map/mi,mnp->inp/dot_general | solution.py:91
  15.4 2.7 %copy.63 = bf16[96,48,256]{2,1,0:T(8,128)(2,1)} copy(bf16[96,48,256]{2,0,1:T(8,128)(2,1)S(1)} %fusion) | data formatting | bytes 4718592 | tf_op jit(solution)/shard_map/mi,mnp->inp/dot_general | solution.py:91
  18.2 3.2 %fusion.4 = bf16[96,32,256]{2,0,1:T(8,128)(2,1)S(1)} fusion(bf16[300,32,256]{2,1,0:T(8,128)(2,1)S(1)} %slice-done.1, bf16[300,96]{0,1:T(8,128)(2,1)S(1)} %get-tuple-element.36), kind=kOutput, calls=%fused_computation.5 | convolution fusion | flops 471859200 | bytes 6545664 | tf_op jit(solution)/shard_map/mi,mnp->inp/dot_general | solution.py:91
  22.3 3.2 %fusion.11 = bf16[96,30,256]{2,0,1:T(8,128)(2,1)S(1)} fusion(bf16[300,30,256]{2,1,0:T(8,128)(2,1)S(1)} %slice-done.2, bf16[300,96]{0,1:T(8,128)(2,1)S(1)} %get-tuple-element.36), kind=kOutput, calls=%fused_computation.24 | convolution fusion | flops 443105280 | bytes 6140160 | tf_op jit(solution)/shard_map/mi,mnp->inp/dot_general | solution.py:91
  28.9 3.3 %collective-permute-start.21 = (bf16[48,62,128]{2,0,1:T(8,128)(2,1)}, bf16[48,62,128]{2,0,1:T(8,128)(2,1)}, u32[]{:S(2)}, u32[]{:S(2)}) collective-permute-start(bf16[48,62,128]{2,0,1:T(8,128)(2,1)} %copy.39), channel_id=1, source_target_pairs={{0,48},{16,32},{32,16},{48,0},{64,112},{80,96},{96,80},{112,64},{1... | collective-permute-start | bytes 2285576 | tf_op jit(solution)/shard_map/ppermute | solution.py:32
  35.4 1.6 collective-permute-start.3
  38.2 3.3 %collective-permute-start.4 = (bf16[150,576]{1,0:T(8,128)(2,1)}, bf16[150,576]{1,0:T(8,128)(2,1)}, u32[]{:S(2)}, u32[]{:S(2)}) collective-permute-start(bf16[150,576]{1,0:T(8,128)(2,1)} %fusion.40), channel_id=1, source_target_pairs={{0,8},{1,9},{2,10},{3,11},{4,12},{5,13},{6,14},{7,15},{8,0},{9,1},... | collective-permute-start | bytes 518408 | tf_op jit(solution)/shard_map/ppermute | solution.py:103
  41.5 2.4 %slice.244 = bf16[48,48,256]{2,1,0:T(8,128)(2,1)} slice(bf16[96,48,256]{2,1,0:T(8,128)(2,1)} %copy.63), slice={[48:96], [0:48], [0:256]} | slice | bytes 2359296 | tf_op jit(solution)/shard_map/slice | solution.py:60
  45.5 3.8 %collective-permute-start.5 = (bf16[150,576]{1,0:T(8,128)(2,1)S(1)}, bf16[150,576]{1,0:T(8,128)(2,1)S(1)}, u32[]{:S(2)}, u32[]{:S(2)}) collective-permute-start(bf16[150,576]{1,0:T(8,128)(2,1)S(1)} %fusion.41), channel_id=1, source_target_pairs={{0,12},{1,13},{2,14},{3,15},{4,0},{5,1},{6,2},{7,3},{8,4},{9,5},{1... | collective-permute-start | bytes 518408 | tf_op jit(solution)/shard_map/ppermute | solution.py:103
  49.3 10.2 %collective-permute-done.13 = bf16[48,40,128]{2,1,0:T(8,128)(2,1)} collective-permute-done((bf16[48,40,128]{2,1,0:T(8,128)(2,1)}, bf16[48,40,128]{2,1,0:T(8,128)(2,1)}, u32[]{:S(2)}, u32[]{:S(2)}) %collective-permute-start.13) | collective-permute-done | bytes 491552 | tf_op jit(solution)/shard_map/ppermute | solution.py:32
  59.4 3.2 %collective-permute-start = (bf16[48,48,256]{2,1,0:T(8,128)(2,1)}, bf16[48,48,256]{2,1,0:T(8,128)(2,1)S(1)}, u32[]{:S(2)}, u32[]{:S(2)}) collective-permute-start(bf16[48,48,256]{2,1,0:T(8,128)(2,1)} %slice.244), channel_id=1, source_target_pairs={{0,64},{16,80},{32,96},{48,112},{64,0},{80,16},{96,32},{112,48},{1... | collective-permute-start | bytes 3538952 | tf_op jit(solution)/shard_map/ppermute | solution.py:32
  64.8 2.5 %collective-permute-start.12 = (bf16[24,40,128]{2,1,0:T(8,128)(2,1)S(1)}, bf16[24,40,128]{2,1,0:T(8,128)(2,1)S(1)}, u32[]{:S(2)}, u32[]{:S(2)}) collective-permute-start(bf16[24,40,128]{2,1,0:T(8,128)(2,1)S(1)} %add_convert_fusion.3), channel_id=1, source_target_pairs={{0,48},{16,32},{32,16},{48,0},{64,112},{80,96},{96,80},{112,64},{1... | collective-permute-start | bytes 737288 | tf_op jit(solution)/shard_map/ppermute | solution.py:32
  71.7 1.5 collective-permute-start.19
  78.4 11.5 %collective-permute-done.19 = bf16[48,62,128]{2,0,1:T(8,128)(2,1)S(1)} collective-permute-done((bf16[48,62,128]{2,0,1:T(8,128)(2,1)S(1)}, bf16[48,62,128]{2,0,1:T(8,128)(2,1)S(1)}, u32[]{:S(2)}, u32[]{:S(2)}) %collective-permute-start.19) | collective-permute-done | bytes 761888 | tf_op jit(solution)/shard_map/ppermute | solution.py:32
  91.2 2.7 %collective-permute-start.2 = (bf16[24,48,128]{2,1,0:T(8,128)(2,1)S(1)}, bf16[24,48,128]{2,1,0:T(8,128)(2,1)S(1)}, u32[]{:S(2)}, u32[]{:S(2)}) collective-permute-start(bf16[24,48,128]{2,1,0:T(8,128)(2,1)S(1)} %get-tuple-element.75), channel_id=1, source_target_pairs={{0,48},{16,32},{32,16},{48,0},{64,112},{80,96},{96,80},{112,64},{1... | collective-permute-start | bytes 884744 | tf_op jit(solution)/shard_map/ppermute | solution.py:32
  94.1 1.7 collective-permute-start.16
  95.8 2.5 %collective-permute-done.22 = bf16[24,62,128]{2,1,0:T(8,128)(2,1)S(1)} collective-permute-done((bf16[24,62,128]{2,1,0:T(8,128)(2,1)S(1)}, bf16[24,62,128]{2,1,0:T(8,128)(2,1)S(1)}, u32[]{:S(2)}, u32[]{:S(2)}) %collective-permute-start.22) | collective-permute-done | bytes 380960 | tf_op jit(solution)/shard_map/ppermute | solution.py:32
  98.3 3.6 %collective-permute-start.17 = (bf16[12,40,256]{2,1,0:T(8,128)(2,1)S(1)}, bf16[12,40,256]{2,1,0:T(8,128)(2,1)S(1)}, u32[]{:S(2)}, u32[]{:S(2)}) collective-permute-start(bf16[12,40,256]{2,1,0:T(8,128)(2,1)S(1)} %fusion.65), channel_id=1, source_target_pairs={{0,8},{1,9},{2,10},{3,11},{4,12},{5,13},{6,14},{7,15},{8,0},{9,1},... | collective-permute-start | bytes 737288 | tf_op jit(solution)/shard_map/ppermute | solution.py:118
  102.4 2.3 %collective-permute-done.1 = bf16[24,48,128]{2,1,0:T(8,128)(2,1)S(1)} collective-permute-done((bf16[24,48,128]{2,1,0:T(8,128)(2,1)S(1)}, bf16[24,48,128]{2,1,0:T(8,128)(2,1)S(1)}, u32[]{:S(2)}, u32[]{:S(2)}) %collective-permute-start.1) | collective-permute-done | bytes 294944 | tf_op jit(solution)/shard_map/ppermute | solution.py:32
  105.4 5.2 %collective-permute-done.6 = bf16[12,48,128]{2,1,0:T(8,128)(2,1)S(1)} collective-permute-done((bf16[12,48,128]{2,1,0:T(8,128)(2,1)S(1)}, bf16[12,48,128]{2,1,0:T(8,128)(2,1)S(1)}, u32[]{:S(2)}, u32[]{:S(2)}) %collective-permute-start.6) | collective-permute-done | bytes 147488 | tf_op jit(solution)/shard_map/ppermute | solution.py:32
  110.8 3.7 %collective-permute-start.10 = (bf16[12,48,256]{2,1,0:T(8,128)(2,1)S(1)}, bf16[12,48,256]{2,1,0:T(8,128)(2,1)S(1)}, u32[]{:S(2)}, u32[]{:S(2)}) collective-permute-start(bf16[12,48,256]{2,1,0:T(8,128)(2,1)S(1)} %pad_maximum_fusion.4), channel_id=1, source_target_pairs={{0,12},{1,13},{2,14},{3,15},{4,0},{5,1},{6,2},{7,3},{8,4},{9,5},{1... | collective-permute-start | bytes 884744 | tf_op jit(solution)/shard_map/ppermute | solution.py:118
  116.9 1.8 collective-permute-done.23
  118.8 1.6 collective-permute-start.24
  120.4 3.4 %collective-permute-start.25 = (bf16[12,62,256]{2,1,0:T(8,128)(2,1)S(1)}, bf16[12,62,256]{2,1,0:T(8,128)(2,1)S(1)}, u32[]{:S(2)}, u32[]{:S(2)}) collective-permute-start(bf16[12,62,256]{2,1,0:T(8,128)(2,1)S(1)} %fusion.55), channel_id=1, source_target_pairs={{0,8},{1,9},{2,10},{3,11},{4,12},{5,13},{6,14},{7,15},{8,0},{9,1},... | collective-permute-start | bytes 1142792 | tf_op jit(solution)/shard_map/ppermute | solution.py:118
  125.9 12.6 %collective-permute-done.24 = bf16[12,62,256]{2,1,0:T(8,128)(2,1)S(1)} collective-permute-done((bf16[12,62,256]{2,1,0:T(8,128)(2,1)S(1)}, bf16[12,62,256]{2,1,0:T(8,128)(2,1)S(1)}, u32[]{:S(2)}, u32[]{:S(2)}) %collective-permute-start.24) | collective-permute-done | bytes 380960 | tf_op jit(solution)/shard_map/ppermute | solution.py:118
  138.5 3.1 %collective-permute-done.25 = bf16[12,62,256]{2,1,0:T(8,128)(2,1)S(1)} collective-permute-done((bf16[12,62,256]{2,1,0:T(8,128)(2,1)S(1)}, bf16[12,62,256]{2,1,0:T(8,128)(2,1)S(1)}, u32[]{:S(2)}, u32[]{:S(2)}) %collective-permute-start.25) | collective-permute-done | bytes 380960 | tf_op jit(solution)/shard_map/ppermute | solution.py:118
  141.6 1.7 add_bitcast_fusion
  143.5 6.8 %collective-permute-start.27 = (bf16[12,288,256]{2,1,0:T(8,128)(2,1)S(1)}, bf16[12,288,256]{2,1,0:T(8,128)(2,1)S(1)}, u32[]{:S(2)}, u32[]{:S(2)}) collective-permute-start(bf16[12,288,256]{2,1,0:T(8,128)(2,1)S(1)} %slice.352), channel_id=1, source_target_pairs={{0,1},{1,0},{2,3},{3,2},{4,5},{5,4},{6,7},{7,6},{8,9},{9,8},{10,11... | collective-permute-start | bytes 5308424 | tf_op jit(solution)/shard_map/ppermute | solution.py:121
  150.3 3.3 %collective-permute-done.27 = bf16[12,288,256]{2,1,0:T(8,128)(2,1)S(1)} collective-permute-done((bf16[12,288,256]{2,1,0:T(8,128)(2,1)S(1)}, bf16[12,288,256]{2,1,0:T(8,128)(2,1)S(1)}, u32[]{:S(2)}, u32[]{:S(2)}) %collective-permute-start.27) | collective-permute-done | bytes 1769504 | tf_op jit(solution)/shard_map/ppermute | solution.py:121
  155.4 19.5 %collective-permute-done.28 = bf16[12,144,256]{2,1,0:T(8,128)(2,1)S(1)} collective-permute-done((bf16[12,144,256]{2,1,0:T(8,128)(2,1)S(1)}, bf16[12,144,256]{2,1,0:T(8,128)(2,1)S(1)}, u32[]{:S(2)}, u32[]{:S(2)}) %collective-permute-start.28) | collective-permute-done | bytes 884768 | tf_op jit(solution)/shard_map/ppermute | solution.py:122
  (118 shorter events, 34.7 us)
Async XLA Ops:
  0.0 34.2 %copy-start = (bf16[150,2304]{1,0:T(8,128)(2,1)S(1)}, bf16[150,2304]{1,0:T(8,128)(2,1)}, u32[]{:S(2)}) copy-start(bf16[150,2304]{1,0:T(8,128)(2,1)} %param.6) | copy-start | bytes 2073604
  28.9 47.7 %collective-permute-start.21 = (bf16[48,62,128]{2,0,1:T(8,128)(2,1)}, bf16[48,62,128]{2,0,1:T(8,128)(2,1)}, u32[]{:S(2)}, u32[]{:S(2)}) collective-permute-start(bf16[48,62,128]{2,0,1:T(8,128)(2,1)} %copy.39), channel_id=1, source_target_pairs={{0,48},{16,32},{32,16},{48,0},{64,112},{80,96},{96,80},{112,64},{1... | collective-permute-start | bytes 2285576 | tf_op jit(solution)/shard_map/ppermute | solution.py:32
  33.4 12.1 %collective-permute-start.11 = (bf16[48,40,128]{2,1,0:T(8,128)(2,1)}, bf16[48,40,128]{2,1,0:T(8,128)(2,1)S(1)}, u32[]{:S(2)}, u32[]{:S(2)}) collective-permute-start(bf16[48,40,128]{2,1,0:T(8,128)(2,1)} %get-tuple-element.74), channel_id=1, source_target_pairs={{0,16},{16,0},{32,48},{48,32},{64,80},{80,64},{96,112},{112,96},{1... | collective-permute-start | bytes 1474568 | tf_op jit(solution)/shard_map/ppermute | solution.py:32
  33.4 26.1 %collective-permute-start.13 = (bf16[48,40,128]{2,1,0:T(8,128)(2,1)}, bf16[48,40,128]{2,1,0:T(8,128)(2,1)}, u32[]{:S(2)}, u32[]{:S(2)}) collective-permute-start(bf16[48,40,128]{2,1,0:T(8,128)(2,1)} %get-tuple-element.73), channel_id=1, source_target_pairs={{0,48},{16,32},{32,16},{48,0},{64,112},{80,96},{96,80},{112,64},{1... | collective-permute-start | bytes 1474568 | tf_op jit(solution)/shard_map/ppermute | solution.py:32
  35.4 29.4 %collective-permute-start.3 = (bf16[150,576]{1,0:T(8,128)(2,1)}, bf16[150,576]{1,0:T(8,128)(2,1)}, u32[]{:S(2)}, u32[]{:S(2)}) collective-permute-start(bf16[150,576]{1,0:T(8,128)(2,1)} %fusion.39), channel_id=1, source_target_pairs={{0,4},{1,5},{2,6},{3,7},{4,8},{5,9},{6,10},{7,11},{8,12},{9,13},{1... | collective-permute-start | bytes 518408 | tf_op jit(solution)/shard_map/ppermute | solution.py:103
  38.2 29.2 %collective-permute-start.4 = (bf16[150,576]{1,0:T(8,128)(2,1)}, bf16[150,576]{1,0:T(8,128)(2,1)}, u32[]{:S(2)}, u32[]{:S(2)}) collective-permute-start(bf16[150,576]{1,0:T(8,128)(2,1)} %fusion.40), channel_id=1, source_target_pairs={{0,8},{1,9},{2,10},{3,11},{4,12},{5,13},{6,14},{7,15},{8,0},{9,1},... | collective-permute-start | bytes 518408 | tf_op jit(solution)/shard_map/ppermute | solution.py:103
  43.8 23.5 %copy-start.3 = (bf16[96,30,256]{2,1,0:T(8,128)(2,1)S(1)}, bf16[96,30,256]{2,1,0:T(8,128)(2,1)}, u32[]{:S(2)}) copy-start(bf16[96,30,256]{2,1,0:T(8,128)(2,1)} %copy-done.2) | copy-start | bytes 4423684
  45.5 26.2 %collective-permute-start.5 = (bf16[150,576]{1,0:T(8,128)(2,1)S(1)}, bf16[150,576]{1,0:T(8,128)(2,1)S(1)}, u32[]{:S(2)}, u32[]{:S(2)}) collective-permute-start(bf16[150,576]{1,0:T(8,128)(2,1)S(1)} %fusion.41), channel_id=1, source_target_pairs={{0,12},{1,13},{2,14},{3,15},{4,0},{5,1},{6,2},{7,3},{8,4},{9,5},{1... | collective-permute-start | bytes 518408 | tf_op jit(solution)/shard_map/ppermute | solution.py:103
  59.4 31.1 %collective-permute-start = (bf16[48,48,256]{2,1,0:T(8,128)(2,1)}, bf16[48,48,256]{2,1,0:T(8,128)(2,1)S(1)}, u32[]{:S(2)}, u32[]{:S(2)}) collective-permute-start(bf16[48,48,256]{2,1,0:T(8,128)(2,1)} %slice.244), channel_id=1, source_target_pairs={{0,64},{16,80},{32,96},{48,112},{64,0},{80,16},{96,32},{112,48},{1... | collective-permute-start | bytes 3538952 | tf_op jit(solution)/shard_map/ppermute | solution.py:32
  64.8 10.3 %collective-permute-start.12 = (bf16[24,40,128]{2,1,0:T(8,128)(2,1)S(1)}, bf16[24,40,128]{2,1,0:T(8,128)(2,1)S(1)}, u32[]{:S(2)}, u32[]{:S(2)}) collective-permute-start(bf16[24,40,128]{2,1,0:T(8,128)(2,1)S(1)} %add_convert_fusion.3), channel_id=1, source_target_pairs={{0,48},{16,32},{32,16},{48,0},{64,112},{80,96},{96,80},{112,64},{1... | collective-permute-start | bytes 737288 | tf_op jit(solution)/shard_map/ppermute | solution.py:32
  67.4 7.7 %collective-permute-start.14 = (bf16[24,40,128]{2,1,0:T(8,128)(2,1)S(1)}, bf16[24,40,128]{2,1,0:T(8,128)(2,1)S(1)}, u32[]{:S(2)}, u32[]{:S(2)}) collective-permute-start(bf16[24,40,128]{2,1,0:T(8,128)(2,1)S(1)} %add_convert_fusion.2), channel_id=1, source_target_pairs={{0,16},{16,0},{32,48},{48,32},{64,80},{80,64},{96,112},{112,96},{1... | collective-permute-start | bytes 737288 | tf_op jit(solution)/shard_map/ppermute | solution.py:32
  71.7 18.1 %collective-permute-start.19 = (bf16[48,62,128]{2,0,1:T(8,128)(2,1)S(1)}, bf16[48,62,128]{2,0,1:T(8,128)(2,1)S(1)}, u32[]{:S(2)}, u32[]{:S(2)}) collective-permute-start(bf16[48,62,128]{2,0,1:T(8,128)(2,1)S(1)} %copy.37), channel_id=1, source_target_pairs={{0,16},{16,0},{32,48},{48,32},{64,80},{80,64},{96,112},{112,96},{1... | collective-permute-start | bytes 2285576 | tf_op jit(solution)/shard_map/ppermute | solution.py:32
  76.5 17.5 %collective-permute-start.15 = (bf16[12,40,256]{2,1,0:T(8,128)(2,1)S(1)}, bf16[12,40,256]{2,1,0:T(8,128)(2,1)S(1)}, u32[]{:S(2)}, u32[]{:S(2)}) collective-permute-start(bf16[12,40,256]{2,1,0:T(8,128)(2,1)S(1)} %fusion.66), channel_id=1, source_target_pairs={{0,64},{16,80},{32,96},{48,112},{64,0},{80,16},{96,32},{112,48},{1... | collective-permute-start | bytes 737288 | tf_op jit(solution)/shard_map/ppermute | solution.py:32
  78.3 20.0 %collective-permute-start.22 = (bf16[24,62,128]{2,1,0:T(8,128)(2,1)S(1)}, bf16[24,62,128]{2,1,0:T(8,128)(2,1)S(1)}, u32[]{:S(2)}, u32[]{:S(2)}) collective-permute-start(bf16[24,62,128]{2,1,0:T(8,128)(2,1)S(1)} %add_convert_fusion), channel_id=1, source_target_pairs={{0,16},{16,0},{32,48},{48,32},{64,80},{80,64},{96,112},{112,96},{1... | collective-permute-start | bytes 1142792 | tf_op jit(solution)/shard_map/ppermute | solution.py:32
  90.2 11.7 %collective-permute-start.20 = (bf16[24,62,128]{2,1,0:T(8,128)(2,1)S(1)}, bf16[24,62,128]{2,1,0:T(8,128)(2,1)S(1)}, u32[]{:S(2)}, u32[]{:S(2)}) collective-permute-start(bf16[24,62,128]{2,1,0:T(8,128)(2,1)S(1)} %add_convert_fusion.1), channel_id=1, source_target_pairs={{0,48},{16,32},{32,16},{48,0},{64,112},{80,96},{96,80},{112,64},{1... | collective-permute-start | bytes 1142792 | tf_op jit(solution)/shard_map/ppermute | solution.py:32
  91.1 13.5 %collective-permute-start.1 = (bf16[24,48,128]{2,1,0:T(8,128)(2,1)S(1)}, bf16[24,48,128]{2,1,0:T(8,128)(2,1)S(1)}, u32[]{:S(2)}, u32[]{:S(2)}) collective-permute-start(bf16[24,48,128]{2,1,0:T(8,128)(2,1)S(1)} %get-tuple-element.76), channel_id=1, source_target_pairs={{0,16},{16,0},{32,48},{48,32},{64,80},{80,64},{96,112},{112,96},{1... | collective-permute-start | bytes 884744 | tf_op jit(solution)/shard_map/ppermute | solution.py:32
  91.2 13.4 %collective-permute-start.2 = (bf16[24,48,128]{2,1,0:T(8,128)(2,1)S(1)}, bf16[24,48,128]{2,1,0:T(8,128)(2,1)S(1)}, u32[]{:S(2)}, u32[]{:S(2)}) collective-permute-start(bf16[24,48,128]{2,1,0:T(8,128)(2,1)S(1)} %get-tuple-element.75), channel_id=1, source_target_pairs={{0,48},{16,32},{32,16},{48,0},{64,112},{80,96},{96,80},{112,64},{1... | collective-permute-start | bytes 884744 | tf_op jit(solution)/shard_map/ppermute | solution.py:32
  94.1 20.5 %collective-permute-start.16 = (bf16[12,40,256]{2,1,0:T(8,128)(2,1)S(1)}, bf16[12,40,256]{2,1,0:T(8,128)(2,1)S(1)}, u32[]{:S(2)}, u32[]{:S(2)}) collective-permute-start(bf16[12,40,256]{2,1,0:T(8,128)(2,1)S(1)} %fusion.65), channel_id=1, source_target_pairs={{0,4},{1,5},{2,6},{3,7},{4,8},{5,9},{6,10},{7,11},{8,12},{9,13},{1... | collective-permute-start | bytes 737288 | tf_op jit(solution)/shard_map/ppermute | solution.py:118
  98.3 16.2 %collective-permute-start.17 = (bf16[12,40,256]{2,1,0:T(8,128)(2,1)S(1)}, bf16[12,40,256]{2,1,0:T(8,128)(2,1)S(1)}, u32[]{:S(2)}, u32[]{:S(2)}) collective-permute-start(bf16[12,40,256]{2,1,0:T(8,128)(2,1)S(1)} %fusion.65), channel_id=1, source_target_pairs={{0,8},{1,9},{2,10},{3,11},{4,12},{5,13},{6,14},{7,15},{8,0},{9,1},... | collective-permute-start | bytes 737288 | tf_op jit(solution)/shard_map/ppermute | solution.py:118
  101.9 13.9 %collective-permute-start.18 = (bf16[12,40,256]{2,1,0:T(8,128)(2,1)S(1)}, bf16[12,40,256]{2,1,0:T(8,128)(2,1)S(1)}, u32[]{:S(2)}, u32[]{:S(2)}) collective-permute-start(bf16[12,40,256]{2,1,0:T(8,128)(2,1)S(1)} %fusion.65), channel_id=1, source_target_pairs={{0,12},{1,13},{2,14},{3,15},{4,0},{5,1},{6,2},{7,3},{8,4},{9,5},{1... | collective-permute-start | bytes 737288 | tf_op jit(solution)/shard_map/ppermute | solution.py:118
  104.7 5.9 %collective-permute-start.6 = (bf16[12,48,128]{2,1,0:T(8,128)(2,1)S(1)}, bf16[12,48,128]{2,1,0:T(8,128)(2,1)S(1)}, u32[]{:S(2)}, u32[]{:S(2)}) collective-permute-start(bf16[12,48,128]{2,1,0:T(8,128)(2,1)S(1)} %get-tuple-element.70), channel_id=1, source_target_pairs={{0,48},{16,32},{32,16},{48,0},{64,112},{80,96},{96,80},{112,64},{1... | collective-permute-start | bytes 442376 | tf_op jit(solution)/shard_map/ppermute | solution.py:32
  105.0 5.6 %collective-permute-start.7 = (bf16[12,48,128]{2,1,0:T(8,128)(2,1)S(1)}, bf16[12,48,128]{2,1,0:T(8,128)(2,1)S(1)}, u32[]{:S(2)}, u32[]{:S(2)}) collective-permute-start(bf16[12,48,128]{2,1,0:T(8,128)(2,1)S(1)} %get-tuple-element.69), channel_id=1, source_target_pairs={{0,16},{16,0},{32,48},{48,32},{64,80},{80,64},{96,112},{112,96},{1... | collective-permute-start | bytes 442376 | tf_op jit(solution)/shard_map/ppermute | solution.py:32
  110.6 8.1 %collective-permute-start.23 = (bf16[12,62,256]{2,1,0:T(8,128)(2,1)S(1)}, bf16[12,62,256]{2,1,0:T(8,128)(2,1)S(1)}, u32[]{:S(2)}, u32[]{:S(2)}) collective-permute-start(bf16[12,62,256]{2,1,0:T(8,128)(2,1)S(1)} %fusion.58), channel_id=1, source_target_pairs={{0,64},{16,80},{32,96},{48,112},{64,0},{80,16},{96,32},{112,48},{1... | collective-permute-start | bytes 1142792 | tf_op jit(solution)/shard_map/ppermute | solution.py:32
  110.8 13.0 %collective-permute-start.10 = (bf16[12,48,256]{2,1,0:T(8,128)(2,1)S(1)}, bf16[12,48,256]{2,1,0:T(8,128)(2,1)S(1)}, u32[]{:S(2)}, u32[]{:S(2)}) collective-permute-start(bf16[12,48,256]{2,1,0:T(8,128)(2,1)S(1)} %pad_maximum_fusion.4), channel_id=1, source_target_pairs={{0,12},{1,13},{2,14},{3,15},{4,0},{5,1},{6,2},{7,3},{8,4},{9,5},{1... | collective-permute-start | bytes 884744 | tf_op jit(solution)/shard_map/ppermute | solution.py:118
  114.5 10.2 %collective-permute-start.8 = (bf16[12,48,256]{2,1,0:T(8,128)(2,1)S(1)}, bf16[12,48,256]{2,1,0:T(8,128)(2,1)S(1)}, u32[]{:S(2)}, u32[]{:S(2)}) collective-permute-start(bf16[12,48,256]{2,1,0:T(8,128)(2,1)S(1)} %pad_maximum_fusion.4), channel_id=1, source_target_pairs={{0,4},{1,5},{2,6},{3,7},{4,8},{5,9},{6,10},{7,11},{8,12},{9,13},{1... | collective-permute-start | bytes 884744 | tf_op jit(solution)/shard_map/ppermute | solution.py:118
  114.5 10.2 %collective-permute-start.9 = (bf16[12,48,256]{2,1,0:T(8,128)(2,1)S(1)}, bf16[12,48,256]{2,1,0:T(8,128)(2,1)S(1)}, u32[]{:S(2)}, u32[]{:S(2)}) collective-permute-start(bf16[12,48,256]{2,1,0:T(8,128)(2,1)S(1)} %pad_maximum_fusion.4), channel_id=1, source_target_pairs={{0,8},{1,9},{2,10},{3,11},{4,12},{5,13},{6,14},{7,15},{8,0},{9,1},... | collective-permute-start | bytes 884744 | tf_op jit(solution)/shard_map/ppermute | solution.py:118
  118.8 19.6 %collective-permute-start.24 = (bf16[12,62,256]{2,1,0:T(8,128)(2,1)S(1)}, bf16[12,62,256]{2,1,0:T(8,128)(2,1)S(1)}, u32[]{:S(2)}, u32[]{:S(2)}) collective-permute-start(bf16[12,62,256]{2,1,0:T(8,128)(2,1)S(1)} %fusion.55), channel_id=1, source_target_pairs={{0,4},{1,5},{2,6},{3,7},{4,8},{5,9},{6,10},{7,11},{8,12},{9,13},{1... | collective-permute-start | bytes 1142792 | tf_op jit(solution)/shard_map/ppermute | solution.py:118
  120.4 21.2 %collective-permute-start.25 = (bf16[12,62,256]{2,1,0:T(8,128)(2,1)S(1)}, bf16[12,62,256]{2,1,0:T(8,128)(2,1)S(1)}, u32[]{:S(2)}, u32[]{:S(2)}) collective-permute-start(bf16[12,62,256]{2,1,0:T(8,128)(2,1)S(1)} %fusion.55), channel_id=1, source_target_pairs={{0,8},{1,9},{2,10},{3,11},{4,12},{5,13},{6,14},{7,15},{8,0},{9,1},... | collective-permute-start | bytes 1142792 | tf_op jit(solution)/shard_map/ppermute | solution.py:118
  123.8 17.8 %collective-permute-start.26 = (bf16[12,62,256]{2,1,0:T(8,128)(2,1)S(1)}, bf16[12,62,256]{2,1,0:T(8,128)(2,1)S(1)}, u32[]{:S(2)}, u32[]{:S(2)}) collective-permute-start(bf16[12,62,256]{2,1,0:T(8,128)(2,1)S(1)} %fusion.55), channel_id=1, source_target_pairs={{0,12},{1,13},{2,14},{3,15},{4,0},{5,1},{6,2},{7,3},{8,4},{9,5},{1... | collective-permute-start | bytes 1142792 | tf_op jit(solution)/shard_map/ppermute | solution.py:118
  143.5 31.4 %copy-start.9 = (s32[256]{0:T(256)S(1)}, s32[256]{0:T(256)}, u32[]{:S(2)}) copy-start(s32[256]{0:T(256)} %param.7) | copy-start | bytes 3076
  143.5 10.2 %collective-permute-start.27 = (bf16[12,288,256]{2,1,0:T(8,128)(2,1)S(1)}, bf16[12,288,256]{2,1,0:T(8,128)(2,1)S(1)}, u32[]{:S(2)}, u32[]{:S(2)}) collective-permute-start(bf16[12,288,256]{2,1,0:T(8,128)(2,1)S(1)} %slice.352), channel_id=1, source_target_pairs={{0,1},{1,0},{2,3},{3,2},{4,5},{5,4},{6,7},{7,6},{8,9},{9,8},{10,11... | collective-permute-start | bytes 5308424 | tf_op jit(solution)/shard_map/ppermute | solution.py:121
  154.0 20.9 %collective-permute-start.28 = (bf16[12,144,256]{2,1,0:T(8,128)(2,1)S(1)}, bf16[12,144,256]{2,1,0:T(8,128)(2,1)S(1)}, u32[]{:S(2)}, u32[]{:S(2)}) collective-permute-start(bf16[12,144,256]{2,1,0:T(8,128)(2,1)S(1)} %fusion.8), channel_id=1, source_target_pairs={{0,2},{1,3},{2,0},{3,1},{4,6},{5,7},{6,4},{7,5},{8,10},{9,11},{10,... | collective-permute-start | bytes 2654216 | tf_op jit(solution)/shard_map/ppermute | solution.py:122
  (14 other events, 123.7 us)

commit v3 on v2

v3 whole, which is shorter than its diff:
```python
import jax
import jax.numpy as jnp
from jax import lax
from jax.experimental.layout import Layout, with_layout_constraint
from jax.sharding import PartitionSpec as P


F32, BF16 = jnp.float32, jnp.bfloat16
B = 12
A_BLK = 144
H = 128
CHUNKS = {"p": (0, 48), "r": (48, 104), "q": (104, 150)}


def row_perm(mask):
    return [(i, i ^ mask) for i in range(8)]


def col_xor(mask):
    return [(i, i ^ mask) for i in range(16)]


def rowmajor(v):
    return with_layout_constraint(v, Layout(major_to_minor=tuple(range(v.ndim))))


def row(v, mask):
    return lax.ppermute(v, "row", row_perm(mask))


def select_cols(mat, source):
    hot = (lax.broadcasted_iota(jnp.int32, (mat.shape[1], source.shape[0]), 0) == source[None, :]).astype(BF16)
    return jnp.dot(mat, hot, preferred_element_type=F32).astype(BF16)


def gather_z(half):
    return jnp.concatenate([half] + [lax.ppermute(half, "col", col_xor(4 * k)) for k in (1, 3, 2)], axis=1)


def f32(v):
    return v.astype(F32)


def x_first(d, cols):
    a1 = row(d[2 * B : 6 * B, :, :H], 1)
    b1 = row(d[4 * B :, :, H:], 3)
    da, a1 = lax.optimization_barrier((d, a1))
    a2 = row((f32(da[6 * B :, :, :H]) + a1[2 * B :]).astype(BF16), 3)
    db, b1 = lax.optimization_barrier((d, b1))
    b2 = row((f32(db[2 * B : 4 * B, :, H:]) + b1[: 2 * B]).astype(BF16), 1)
    d, a2, b2, *cols = lax.optimization_barrier((d, a2, b2, *cols))
    own = jnp.concatenate(
        [f32(d[: 2 * B, :, :H]) + a1[: 2 * B] + a2, f32(d[: 2 * B, :, H:]) + b1[2 * B :] + b2], axis=2
    )
    y = row(own[B:].astype(BF16), 4)
    return (own[:B] + y).astype(BF16), *cols


def local(integrals, occ_coef, virt_coef, pair_index):
    r = lax.axis_index("row")
    c = lax.axis_index("col")
    yh, x = r // 4, r % 4
    z, yl, core = c // 4, (c // 2) % 2, c % 2

    pos = jnp.arange(96, dtype=jnp.int32)
    source = ((yh ^ ((pos // B) % 2)) * 4 + (x ^ (pos // (2 * B)))) * B + pos % B
    occ = select_cols(occ_coef, source)

    products, held = {}, occ
    for name, (lo, hi) in CHUNKS.items():
        weights = lax.optimization_barrier((occ, held))[0]
        d = jnp.einsum("mi,mnp->inp", weights, integrals[:, lo:hi], preferred_element_type=F32).astype(BF16)
        products[name] = held = rowmajor(d)
    products["r"], virt_coef, _ = lax.optimization_barrier((products["r"], virt_coef, held))

    apos = jnp.arange(4 * A_BLK, dtype=jnp.int32)
    a_source = ((yl ^ ((apos // A_BLK) % 2)) * 2 + (core ^ (apos // (2 * A_BLK)))) * A_BLK + apos % A_BLK
    virt = {}
    for k in (0, 1, 3, 2):
        v = lax.dynamic_slice_in_dim(virt_coef, (z ^ k) * 4 * A_BLK, 4 * A_BLK, axis=1)
        v = select_cols(v, a_source)
        virt[k] = v if k == 0 else lax.ppermute(v, "col", col_xor(4 * k))

    cols = {n: jnp.concatenate([virt[k][lo:hi] for k in (0, 1, 3, 2)], axis=0) for n, (lo, hi) in CHUNKS.items()}

    halves = {}
    for name, d in products.items():
        if name == "q":
            halves[name], *tied = x_first(d, list(cols.values()))
            cols = dict(zip(cols, tied))
        else:
            halves[name] = x_first(d, [])[0]
    acc = 0.0
    for name, half in halves.items():
        acc = acc + jnp.einsum("inp,na->iap", gather_z(half), cols[name], preferred_element_type=F32)

    r4 = lax.ppermute(acc[:, 2 * A_BLK :].astype(BF16), "col", col_xor(1))
    r5 = lax.ppermute((acc[:, A_BLK : 2 * A_BLK] + r4[:, A_BLK:]).astype(BF16), "col", col_xor(2))
    slab = (acc[:, :A_BLK] + r4[:, :A_BLK] + r5).astype(BF16)
    hot = (lax.broadcasted_iota(jnp.int32, (256, 256), 0) == pair_index[None, :]).astype(BF16)
    return jnp.einsum("iap,pk->iak", slab, hot, preferred_element_type=F32).astype(BF16)


def solution(mesh):
    return jax.shard_map(
        local,
        mesh=mesh,
        in_specs=(P("row", "col", None), P("row", None), P("col", None), P()),
        out_specs=P("row", "col", None),
        check_vma=False,
    )
```

time: 177 us -> 178 us (level)
  waiting for transfers between devices: 73 us -> 81.4 us
  starting transfers between devices: 48.4 us -> 43.6 us
  other arithmetic: 6.21 us -> 2 us
  local copies, waits for them, and re-layouts: 25.6 us -> 29.4 us
  matrix products: 22.6 us -> 20.1 us
    ppermute x12, starting transfers between devices: 25 us -> 15.3 us  [the longest x9 9.48 us: gather_z(): lax.ppermute(half, 'col', col_xor(4 * k))]
    ppermute x12, waiting for transfers between devices: 16.1 us -> 22.7 us  [the longest x9 22.7 us: gather_z(): lax.ppermute(half, 'col', col_xor(4 * k))]
    ppermute x15, starting transfers between devices: 15.2 us -> 21.2 us  [row(): return lax.ppermute(v, 'row', row_perm(mask))]
    dot_general x4 -> x3, matrix products: 13.7 us -> 10.8 us  [local(): jnp.einsum('mi,mnp->inp', weights, integrals[:, lo:hi], preferred_element...]
    convert_element_type x1, local copies, waits for them, and re-layouts: 0.83 us -> 2.7 us  [local(): jnp.einsum('mi,mnp->inp', weights, integrals[:, lo:hi], preferred_element...]
    slice x7 -> x5, local copies, waits for them, and re-layouts: 5.9 us -> 6.59 us  [local(): integrals[:, lo:hi]]
    dot_general x3 -> x2, local copies, waits for them, and re-layouts: 4.74 us -> 4.34 us  [local(): jnp.einsum('mi,mnp->inp', weights, integrals[:, lo:hi], preferred_element...]
    slice x19 -> x12, local copies, waits for them, and re-layouts: 7.6 us -> 7.7 us  [local(): virt[k][lo:hi]]
where the time goes in v3:
time: 178 us; the launch traced here: 177 us
  waiting for transfers between devices  81.4 us (46%)
  starting transfers between devices  43.6 us (24%)
  local copies, waits for them, and re-layouts  29.4 us (17%)
  matrix products  20.1 us (11%)
  other arithmetic  2 us (1%)
    ppermute x15, waiting for transfers between devices, row(): return lax.ppermute(v, 'row', row_perm(mask))  35.8 us
    ppermute x9, waiting for transfers between devices, gather_z(): lax.ppermute(half, 'col', col_xor(4 * k))  22.7 us
    ppermute x15, starting transfers between devices, row(): return lax.ppermute(v, 'row', row_perm(mask))  21.2 us
    ppermute x1, waiting for transfers between devices, local(): lax.ppermute((acc[:, A_BLK:2 * A_BLK] + r4[:, A_BLK:]).astype(BF16), 'col...  19.6 us
    dot_general x3, matrix products, local(): jnp.einsum('mi,mnp->inp', weights, integrals[:, lo:hi], preferred_element...  10.8 us
    ppermute x9, starting transfers between devices, gather_z(): lax.ppermute(half, 'col', col_xor(4 * k))  9.48 us
    slice x12, local copies, waits for them, and re-layouts, local(): virt[k][lo:hi]  7.7 us
    slice x5, local copies, waits for them, and re-layouts, local(): integrals[:, lo:hi]  6.59 us
  transfers between devices with their start and end apart: 29, of which 12 were waited for; matrix products, arithmetic and copies ran while one was open for 12% of the time, Pallas kernels for 0%

profile of v3, /device:TPU:1, one launch (start us, length us, event | category | flops | bytes accessed | tf_op | source)
XLA Modules:
  0.0 176.9 jit_solution(17926322421319024324)
XLA Ops:
  0.0 6.6 %slice.172 = bf16[300,48,256]{2,1,0:T(8,128)(2,1)} slice(bf16[300,150,256]{2,1,0:T(8,128)(2,1)} %param.4), slice={[0:300], [0:48], [0:256]} | slice | bytes 14745600 | tf_op jit(solution)/shard_map/slice | solution.py:72
  7.7 6.0 %fusion.2 = bf16[96,48,256]{2,0,1:T(8,128)(2,1)S(1)} fusion(bf16[300,48,256]{2,1,0:T(8,128)(2,1)} %slice.172, bf16[300,96]{0,1:T(8,128)(2,1)S(1)} %fusion.46), kind=kOutput, calls=%fused_computation.2 | convolution fusion | flops 707788800 | bytes 9789696 | tf_op jit(solution)/shard_map/mi,mnp->inp/dot_general | solution.py:72
  13.7 2.8 %copy.49 = bf16[96,48,256]{2,1,0:T(8,128)(2,1)} copy(bf16[96,48,256]{2,0,1:T(8,128)(2,1)S(1)} %fusion.2) | data formatting | bytes 4718592 | tf_op jit(solution)/shard_map/mi,mnp->inp/dot_general | solution.py:72
  16.5 2.2 %fusion = bf16[96,56,256]{2,0,1:T(8,128)(2,1)S(1)} fusion(bf16[300,56,256]{2,1,0:T(8,128)(2,1)S(1)} %slice-done, bf16[300,96]{0,1:T(8,128)(2,1)S(1)} %fusion.46), kind=kOutput, calls=%fused_computation | convolution fusion | flops 825753600 | bytes 11411712 | tf_op jit(solution)/shard_map/mi,mnp->inp/dot_general | solution.py:72
  18.7 1.5 copy.48
  20.2 2.6 %fusion.6 = bf16[96,46,256]{2,0,1:T(8,128)(2,1)S(1)} fusion(bf16[300,46,256]{2,1,0:T(8,128)(2,1)S(1)} %slice-done.1, bf16[300,96]{0,1:T(8,128)(2,1)S(1)} %fusion.46), kind=kOutput, calls=%fused_computation.10 | convolution fusion | flops 679428096 | bytes 9384192 | tf_op jit(solution)/shard_map/mi,mnp->inp/dot_general | solution.py:72
  22.9 2.7 %copy.28 = bf16[96,46,256]{2,1,0:T(8,128)(2,1)} copy(bf16[96,46,256]{2,0,1:T(8,128)(2,1)S(1)} %fusion.6) | data formatting | bytes 4521984 | tf_op jit(solution)/shard_map/convert_element_type | solution.py:72
  26.8 2.5 %collective-permute-start.4 = (bf16[150,576]{1,0:T(8,128)(2,1)}, bf16[150,576]{1,0:T(8,128)(2,1)}, u32[]{:S(2)}, u32[]{:S(2)}) collective-permute-start(bf16[150,576]{1,0:T(8,128)(2,1)} %fusion.33), channel_id=1, source_target_pairs={{0,4},{1,5},{2,6},{3,7},{4,0},{5,1},{6,2},{7,3},{8,12},{9,13},{10,... | collective-permute-start | bytes 518408 | tf_op jit(solution)/shard_map/ppermute | solution.py:82
  30.4 2.2 %collective-permute-start.5 = (bf16[150,576]{1,0:T(8,128)(2,1)}, bf16[150,576]{1,0:T(8,128)(2,1)}, u32[]{:S(2)}, u32[]{:S(2)}) collective-permute-start(bf16[150,576]{1,0:T(8,128)(2,1)} %fusion.34), channel_id=1, source_target_pairs={{0,12},{1,13},{2,14},{3,15},{4,8},{5,9},{6,10},{7,11},{8,4},{9,5},... | collective-permute-start | bytes 518408 | tf_op jit(solution)/shard_map/ppermute | solution.py:82
  37.2 2.5 %collective-permute-start.2 = (bf16[48,46,128]{2,0,1:T(8,128)(2,1)}, bf16[48,46,128]{2,0,1:T(8,128)(2,1)}, u32[]{:S(2)}, u32[]{:S(2)}) collective-permute-start(bf16[48,46,128]{2,0,1:T(8,128)(2,1)} %copy.31), channel_id=1, source_target_pairs={{0,48},{16,32},{32,16},{48,0},{64,112},{80,96},{96,80},{112,64},{1... | collective-permute-start | bytes 1695752 | tf_op jit(solution)/shard_map/ppermute | solution.py:28
  47.8 2.0 %collective-permute-start.9 = (bf16[48,48,128]{2,1,0:T(8,128)(2,1)S(1)}, bf16[48,48,128]{2,1,0:T(8,128)(2,1)S(1)}, u32[]{:S(2)}, u32[]{:S(2)}) collective-permute-start(bf16[48,48,128]{2,1,0:T(8,128)(2,1)S(1)} %get-tuple-element.73), channel_id=1, source_target_pairs={{0,48},{16,32},{32,16},{48,0},{64,112},{80,96},{96,80},{112,64},{1... | collective-permute-start | bytes 1769480 | tf_op jit(solution)/shard_map/ppermute | solution.py:28
  55.6 1.5 collective-permute-start.3
  58.4 20.7 %collective-permute-done.9 = bf16[48,48,128]{2,1,0:T(8,128)(2,1)S(1)} collective-permute-done((bf16[48,48,128]{2,1,0:T(8,128)(2,1)S(1)}, bf16[48,48,128]{2,1,0:T(8,128)(2,1)S(1)}, u32[]{:S(2)}, u32[]{:S(2)}) %collective-permute-start.9) | collective-permute-done | bytes 589856 | tf_op jit(solution)/shard_map/ppermute | solution.py:28
  79.1 2.5 %collective-permute-start.1 = (bf16[24,46,128]{2,1,0:T(8,128)(2,1)S(1)}, bf16[24,46,128]{2,1,0:T(8,128)(2,1)S(1)}, u32[]{:S(2)}, u32[]{:S(2)}) collective-permute-start(bf16[24,46,128]{2,1,0:T(8,128)(2,1)S(1)} %add_convert_fusion.5), channel_id=1, source_target_pairs={{0,48},{16,32},{32,16},{48,0},{64,112},{80,96},{96,80},{112,64},{1... | collective-permute-start | bytes 847880 | tf_op jit(solution)/shard_map/ppermute | solution.py:28
  83.8 3.7 %collective-permute-done.3 = bf16[24,46,128]{2,1,0:T(8,128)(2,1)S(1)} collective-permute-done((bf16[24,46,128]{2,1,0:T(8,128)(2,1)S(1)}, bf16[24,46,128]{2,1,0:T(8,128)(2,1)S(1)}, u32[]{:S(2)}, u32[]{:S(2)}) %collective-permute-start.3) | collective-permute-done | bytes 282656 | tf_op jit(solution)/shard_map/ppermute | solution.py:28
  87.9 3.0 %collective-permute-start.23 = (bf16[12,46,256]{2,1,0:T(8,128)(2,1)S(1)}, bf16[12,46,256]{2,1,0:T(8,128)(2,1)S(1)}, u32[]{:S(2)}, u32[]{:S(2)}) collective-permute-start(bf16[12,46,256]{2,1,0:T(8,128)(2,1)S(1)} %fusion.63), channel_id=1, source_target_pairs={{0,64},{16,80},{32,96},{48,112},{64,0},{80,16},{96,32},{112,48},{1... | collective-permute-start | bytes 847880 | tf_op jit(solution)/shard_map/ppermute | solution.py:28
  90.9 2.9 %collective-permute-done.10 = bf16[24,48,128]{2,1,0:T(8,128)(2,1)S(1)} collective-permute-done((bf16[24,48,128]{2,1,0:T(8,128)(2,1)S(1)}, bf16[24,48,128]{2,1,0:T(8,128)(2,1)S(1)}, u32[]{:S(2)}, u32[]{:S(2)}) %collective-permute-start.10) | collective-permute-done | bytes 294944 | tf_op jit(solution)/shard_map/ppermute | solution.py:28
  94.0 3.0 %collective-permute-start.11 = (bf16[12,48,256]{2,1,0:T(8,128)(2,1)S(1)}, bf16[12,48,256]{2,1,0:T(8,128)(2,1)S(1)}, u32[]{:S(2)}, u32[]{:S(2)}) collective-permute-start(bf16[12,48,256]{2,1,0:T(8,128)(2,1)S(1)} %fusion.64), channel_id=1, source_target_pairs={{0,64},{16,80},{32,96},{48,112},{64,0},{80,16},{96,32},{112,48},{1... | collective-permute-start | bytes 884744 | tf_op jit(solution)/shard_map/ppermute | solution.py:28
  97.0 4.2 %collective-permute-done.18 = bf16[24,56,128]{2,1,0:T(8,128)(2,1)S(1)} collective-permute-done((bf16[24,56,128]{2,1,0:T(8,128)(2,1)S(1)}, bf16[24,56,128]{2,1,0:T(8,128)(2,1)S(1)}, u32[]{:S(2)}, u32[]{:S(2)}) %collective-permute-start.18) | collective-permute-done | bytes 344096 | tf_op jit(solution)/shard_map/ppermute | solution.py:28
  101.4 3.0 %collective-permute-start.19 = (bf16[12,56,256]{2,1,0:T(8,128)(2,1)S(1)}, bf16[12,56,256]{2,1,0:T(8,128)(2,1)S(1)}, u32[]{:S(2)}, u32[]{:S(2)}) collective-permute-start(bf16[12,56,256]{2,1,0:T(8,128)(2,1)S(1)} %fusion.56), channel_id=1, source_target_pairs={{0,64},{16,80},{32,96},{48,112},{64,0},{80,16},{96,32},{112,48},{1... | collective-permute-start | bytes 1032200 | tf_op jit(solution)/shard_map/ppermute | solution.py:28
  104.6 1.9 %collective-permute-start.13 = (bf16[12,48,256]{2,1,0:T(8,128)(2,1)S(1)}, bf16[12,48,256]{2,1,0:T(8,128)(2,1)S(1)}, u32[]{:S(2)}, u32[]{:S(2)}) collective-permute-start(bf16[12,48,256]{2,1,0:T(8,128)(2,1)S(1)} %fusion.62), channel_id=1, source_target_pairs={{0,12},{1,13},{2,14},{3,15},{4,8},{5,9},{6,10},{7,11},{8,4},{9,5},... | collective-permute-start | bytes 884744 | tf_op jit(solution)/shard_map/ppermute | solution.py:37
  108.1 4.3 %collective-permute-done.19 = bf16[12,56,256]{2,1,0:T(8,128)(2,1)S(1)} collective-permute-done((bf16[12,56,256]{2,1,0:T(8,128)(2,1)S(1)}, bf16[12,56,256]{2,1,0:T(8,128)(2,1)S(1)}, u32[]{:S(2)}, u32[]{:S(2)}) %collective-permute-start.19) | collective-permute-done | bytes 344096 | tf_op jit(solution)/shard_map/ppermute | solution.py:28
  112.4 2.5 %collective-permute-start.25 = (bf16[12,46,256]{2,1,0:T(8,128)(2,1)S(1)}, bf16[12,46,256]{2,1,0:T(8,128)(2,1)S(1)}, u32[]{:S(2)}, u32[]{:S(2)}) collective-permute-start(bf16[12,46,256]{2,1,0:T(8,128)(2,1)S(1)} %fusion.59), channel_id=1, source_target_pairs={{0,12},{1,13},{2,14},{3,15},{4,8},{5,9},{6,10},{7,11},{8,4},{9,5},... | collective-permute-start | bytes 847880 | tf_op jit(solution)/shard_map/ppermute | solution.py:37
  115.8 2.5 %collective-permute-start.22 = (bf16[12,56,256]{2,1,0:T(8,128)(2,1)S(1)}, bf16[12,56,256]{2,1,0:T(8,128)(2,1)S(1)}, u32[]{:S(2)}, u32[]{:S(2)}) collective-permute-start(bf16[12,56,256]{2,1,0:T(8,128)(2,1)S(1)} %fusion.55), channel_id=1, source_target_pairs={{0,8},{1,9},{2,10},{3,11},{4,12},{5,13},{6,14},{7,15},{8,0},{9,1},... | collective-permute-start | bytes 1032200 | tf_op jit(solution)/shard_map/ppermute | solution.py:37
  119.4 9.9 %collective-permute-done.20 = bf16[12,56,256]{2,1,0:T(8,128)(2,1)S(1)} collective-permute-done((bf16[12,56,256]{2,1,0:T(8,128)(2,1)S(1)}, bf16[12,56,256]{2,1,0:T(8,128)(2,1)S(1)}, u32[]{:S(2)}, u32[]{:S(2)}) %collective-permute-start.20) | collective-permute-done | bytes 344096 | tf_op jit(solution)/shard_map/ppermute | solution.py:37
  130.0 6.5 %collective-permute-done.21 = bf16[12,56,256]{2,1,0:T(8,128)(2,1)S(1)} collective-permute-done((bf16[12,56,256]{2,1,0:T(8,128)(2,1)S(1)}, bf16[12,56,256]{2,1,0:T(8,128)(2,1)S(1)}, u32[]{:S(2)}, u32[]{:S(2)}) %collective-permute-start.21) | collective-permute-done | bytes 344096 | tf_op jit(solution)/shard_map/ppermute | solution.py:37
  138.0 5.5 %collective-permute-done.26 = bf16[12,46,256]{2,1,0:T(8,128)(2,1)S(1)} collective-permute-done((bf16[12,46,256]{2,1,0:T(8,128)(2,1)S(1)}, bf16[12,46,256]{2,1,0:T(8,128)(2,1)S(1)}, u32[]{:S(2)}, u32[]{:S(2)}) %collective-permute-start.26) | collective-permute-done | bytes 282656 | tf_op jit(solution)/shard_map/ppermute | solution.py:37
  143.5 1.4 add_bitcast_fusion
  145.1 5.8 %collective-permute-start.27 = (bf16[12,288,256]{2,1,0:T(8,128)(2,1)S(1)}, bf16[12,288,256]{2,1,0:T(8,128)(2,1)S(1)}, u32[]{:S(2)}, u32[]{:S(2)}) collective-permute-start(bf16[12,288,256]{2,1,0:T(8,128)(2,1)S(1)} %slice.328), channel_id=1, source_target_pairs={{0,1},{1,0},{2,3},{3,2},{4,5},{5,4},{6,7},{7,6},{8,9},{9,8},{10,11... | collective-permute-start | bytes 5308424 | tf_op jit(solution)/shard_map/ppermute | solution.py:97
  150.9 3.3 %collective-permute-done.27 = bf16[12,288,256]{2,1,0:T(8,128)(2,1)S(1)} collective-permute-done((bf16[12,288,256]{2,1,0:T(8,128)(2,1)S(1)}, bf16[12,288,256]{2,1,0:T(8,128)(2,1)S(1)}, u32[]{:S(2)}, u32[]{:S(2)}) %collective-permute-start.27) | collective-permute-done | bytes 1769504 | tf_op jit(solution)/shard_map/ppermute | solution.py:97
  155.9 19.6 %collective-permute-done.28 = bf16[12,144,256]{2,1,0:T(8,128)(2,1)S(1)} collective-permute-done((bf16[12,144,256]{2,1,0:T(8,128)(2,1)S(1)}, bf16[12,144,256]{2,1,0:T(8,128)(2,1)S(1)}, u32[]{:S(2)}, u32[]{:S(2)}) %collective-permute-start.28) | collective-permute-done | bytes 884768 | tf_op jit(solution)/shard_map/ppermute | solution.py:98
  175.5 1.4 convolution_convert_fusion
  (99 shorter events, 33.9 us)
Async XLA Ops:
  0.0 25.6 %copy-start = (bf16[150,2304]{1,0:T(8,128)(2,1)S(1)}, bf16[150,2304]{1,0:T(8,128)(2,1)}, u32[]{:S(2)}) copy-start(bf16[150,2304]{1,0:T(8,128)(2,1)} %param.6) | copy-start | bytes 2073604
  26.8 15.8 %collective-permute-start.4 = (bf16[150,576]{1,0:T(8,128)(2,1)}, bf16[150,576]{1,0:T(8,128)(2,1)}, u32[]{:S(2)}, u32[]{:S(2)}) collective-permute-start(bf16[150,576]{1,0:T(8,128)(2,1)} %fusion.33), channel_id=1, source_target_pairs={{0,4},{1,5},{2,6},{3,7},{4,0},{5,1},{6,2},{7,3},{8,12},{9,13},{10,... | collective-permute-start | bytes 518408 | tf_op jit(solution)/shard_map/ppermute | solution.py:82
  30.4 14.7 %collective-permute-start.5 = (bf16[150,576]{1,0:T(8,128)(2,1)}, bf16[150,576]{1,0:T(8,128)(2,1)}, u32[]{:S(2)}, u32[]{:S(2)}) collective-permute-start(bf16[150,576]{1,0:T(8,128)(2,1)} %fusion.34), channel_id=1, source_target_pairs={{0,12},{1,13},{2,14},{3,15},{4,8},{5,9},{6,10},{7,11},{8,4},{9,5},... | collective-permute-start | bytes 518408 | tf_op jit(solution)/shard_map/ppermute | solution.py:82
  33.9 13.9 %collective-permute-start.6 = (bf16[150,576]{1,0:T(8,128)(2,1)}, bf16[150,576]{1,0:T(8,128)(2,1)}, u32[]{:S(2)}, u32[]{:S(2)}) collective-permute-start(bf16[150,576]{1,0:T(8,128)(2,1)} %fusion.35), channel_id=1, source_target_pairs={{0,8},{1,9},{2,10},{3,11},{4,12},{5,13},{6,14},{7,15},{8,0},{9,1},... | collective-permute-start | bytes 518408 | tf_op jit(solution)/shard_map/ppermute | solution.py:82
  37.2 17.0 %collective-permute-start.2 = (bf16[48,46,128]{2,0,1:T(8,128)(2,1)}, bf16[48,46,128]{2,0,1:T(8,128)(2,1)}, u32[]{:S(2)}, u32[]{:S(2)}) collective-permute-start(bf16[48,46,128]{2,0,1:T(8,128)(2,1)} %copy.31), channel_id=1, source_target_pairs={{0,48},{16,32},{32,16},{48,0},{64,112},{80,96},{96,80},{112,64},{1... | collective-permute-start | bytes 1695752 | tf_op jit(solution)/shard_map/ppermute | solution.py:28
  40.7 14.9 %collective-permute-start = (bf16[48,46,128]{2,0,1:T(8,128)(2,1)}, bf16[48,46,128]{2,0,1:T(8,128)(2,1)}, u32[]{:S(2)}, u32[]{:S(2)}) collective-permute-start(bf16[48,46,128]{2,0,1:T(8,128)(2,1)} %copy.29), channel_id=1, source_target_pairs={{0,16},{16,0},{32,48},{48,32},{64,80},{80,64},{96,112},{112,96},{1... | collective-permute-start | bytes 1695752 | tf_op jit(solution)/shard_map/ppermute | solution.py:28
  42.6 39.3 %collective-permute-start.17 = (bf16[48,56,128]{2,1,0:T(8,128)(2,1)S(1)}, bf16[48,56,128]{2,1,0:T(8,128)(2,1)S(1)}, u32[]{:S(2)}, u32[]{:S(2)}) collective-permute-start(bf16[48,56,128]{2,1,0:T(8,128)(2,1)S(1)} %get-tuple-element.65), channel_id=1, source_target_pairs={{0,48},{16,32},{32,16},{48,0},{64,112},{80,96},{96,80},{112,64},{1... | collective-permute-start | bytes 2064392 | tf_op jit(solution)/shard_map/ppermute | solution.py:28
  45.2 37.1 %collective-permute-start.15 = (bf16[48,56,128]{2,1,0:T(8,128)(2,1)S(1)}, bf16[48,56,128]{2,1,0:T(8,128)(2,1)S(1)}, u32[]{:S(2)}, u32[]{:S(2)}) collective-permute-start(bf16[48,56,128]{2,1,0:T(8,128)(2,1)S(1)} %get-tuple-element.66), channel_id=1, source_target_pairs={{0,16},{16,0},{32,48},{48,32},{64,80},{80,64},{96,112},{112,96},{1... | collective-permute-start | bytes 2064392 | tf_op jit(solution)/shard_map/ppermute | solution.py:28
  47.8 31.3 %collective-permute-start.9 = (bf16[48,48,128]{2,1,0:T(8,128)(2,1)S(1)}, bf16[48,48,128]{2,1,0:T(8,128)(2,1)S(1)}, u32[]{:S(2)}, u32[]{:S(2)}) collective-permute-start(bf16[48,48,128]{2,1,0:T(8,128)(2,1)S(1)} %get-tuple-element.73), channel_id=1, source_target_pairs={{0,48},{16,32},{32,16},{48,0},{64,112},{80,96},{96,80},{112,64},{1... | collective-permute-start | bytes 1769480 | tf_op jit(solution)/shard_map/ppermute | solution.py:28
  54.2 27.5 %collective-permute-start.7 = (bf16[48,48,128]{2,1,0:T(8,128)(2,1)S(1)}, bf16[48,48,128]{2,1,0:T(8,128)(2,1)S(1)}, u32[]{:S(2)}, u32[]{:S(2)}) collective-permute-start(bf16[48,48,128]{2,1,0:T(8,128)(2,1)S(1)} %get-tuple-element.74), channel_id=1, source_target_pairs={{0,16},{16,0},{32,48},{48,32},{64,80},{80,64},{96,112},{112,96},{1... | collective-permute-start | bytes 1769480 | tf_op jit(solution)/shard_map/ppermute | solution.py:28
  55.6 31.8 %collective-permute-start.3 = (bf16[24,46,128]{2,1,0:T(8,128)(2,1)S(1)}, bf16[24,46,128]{2,1,0:T(8,128)(2,1)S(1)}, u32[]{:S(2)}, u32[]{:S(2)}) collective-permute-start(bf16[24,46,128]{2,1,0:T(8,128)(2,1)S(1)} %add_convert_fusion.4), channel_id=1, source_target_pairs={{0,16},{16,0},{32,48},{48,32},{64,80},{80,64},{96,112},{112,96},{1... | collective-permute-start | bytes 847880 | tf_op jit(solution)/shard_map/ppermute | solution.py:28
  79.1 8.5 %collective-permute-start.1 = (bf16[24,46,128]{2,1,0:T(8,128)(2,1)S(1)}, bf16[24,46,128]{2,1,0:T(8,128)(2,1)S(1)}, u32[]{:S(2)}, u32[]{:S(2)}) collective-permute-start(bf16[24,46,128]{2,1,0:T(8,128)(2,1)S(1)} %add_convert_fusion.5), channel_id=1, source_target_pairs={{0,48},{16,32},{32,16},{48,0},{64,112},{80,96},{96,80},{112,64},{1... | collective-permute-start | bytes 847880 | tf_op jit(solution)/shard_map/ppermute | solution.py:28
  81.7 12.0 %collective-permute-start.10 = (bf16[24,48,128]{2,1,0:T(8,128)(2,1)S(1)}, bf16[24,48,128]{2,1,0:T(8,128)(2,1)S(1)}, u32[]{:S(2)}, u32[]{:S(2)}) collective-permute-start(bf16[24,48,128]{2,1,0:T(8,128)(2,1)S(1)} %add_convert_fusion.2), channel_id=1, source_target_pairs={{0,16},{16,0},{32,48},{48,32},{64,80},{80,64},{96,112},{112,96},{1... | collective-permute-start | bytes 884744 | tf_op jit(solution)/shard_map/ppermute | solution.py:28
  81.9 11.8 %collective-permute-start.8 = (bf16[24,48,128]{2,1,0:T(8,128)(2,1)S(1)}, bf16[24,48,128]{2,1,0:T(8,128)(2,1)S(1)}, u32[]{:S(2)}, u32[]{:S(2)}) collective-permute-start(bf16[24,48,128]{2,1,0:T(8,128)(2,1)S(1)} %add_convert_fusion.3), channel_id=1, source_target_pairs={{0,48},{16,32},{32,16},{48,0},{64,112},{80,96},{96,80},{112,64},{1... | collective-permute-start | bytes 884744 | tf_op jit(solution)/shard_map/ppermute | solution.py:28
  82.3 18.8 %collective-permute-start.18 = (bf16[24,56,128]{2,1,0:T(8,128)(2,1)S(1)}, bf16[24,56,128]{2,1,0:T(8,128)(2,1)S(1)}, u32[]{:S(2)}, u32[]{:S(2)}) collective-permute-start(bf16[24,56,128]{2,1,0:T(8,128)(2,1)S(1)} %add_convert_fusion), channel_id=1, source_target_pairs={{0,16},{16,0},{32,48},{48,32},{64,80},{80,64},{96,112},{112,96},{1... | collective-permute-start | bytes 1032200 | tf_op jit(solution)/shard_map/ppermute | solution.py:28
  87.4 13.7 %collective-permute-start.16 = (bf16[24,56,128]{2,1,0:T(8,128)(2,1)S(1)}, bf16[24,56,128]{2,1,0:T(8,128)(2,1)S(1)}, u32[]{:S(2)}, u32[]{:S(2)}) collective-permute-start(bf16[24,56,128]{2,1,0:T(8,128)(2,1)S(1)} %add_convert_fusion.1), channel_id=1, source_target_pairs={{0,48},{16,32},{32,16},{48,0},{64,112},{80,96},{96,80},{112,64},{1... | collective-permute-start | bytes 1032200 | tf_op jit(solution)/shard_map/ppermute | solution.py:28
  87.9 19.9 %collective-permute-start.23 = (bf16[12,46,256]{2,1,0:T(8,128)(2,1)S(1)}, bf16[12,46,256]{2,1,0:T(8,128)(2,1)S(1)}, u32[]{:S(2)}, u32[]{:S(2)}) collective-permute-start(bf16[12,46,256]{2,1,0:T(8,128)(2,1)S(1)} %fusion.63), channel_id=1, source_target_pairs={{0,64},{16,80},{32,96},{48,112},{64,0},{80,16},{96,32},{112,48},{1... | collective-permute-start | bytes 847880 | tf_op jit(solution)/shard_map/ppermute | solution.py:28
  94.0 10.4 %collective-permute-start.11 = (bf16[12,48,256]{2,1,0:T(8,128)(2,1)S(1)}, bf16[12,48,256]{2,1,0:T(8,128)(2,1)S(1)}, u32[]{:S(2)}, u32[]{:S(2)}) collective-permute-start(bf16[12,48,256]{2,1,0:T(8,128)(2,1)S(1)} %fusion.64), channel_id=1, source_target_pairs={{0,64},{16,80},{32,96},{48,112},{64,0},{80,16},{96,32},{112,48},{1... | collective-permute-start | bytes 884744 | tf_op jit(solution)/shard_map/ppermute | solution.py:28
  101.4 11.0 %collective-permute-start.19 = (bf16[12,56,256]{2,1,0:T(8,128)(2,1)S(1)}, bf16[12,56,256]{2,1,0:T(8,128)(2,1)S(1)}, u32[]{:S(2)}, u32[]{:S(2)}) collective-permute-start(bf16[12,56,256]{2,1,0:T(8,128)(2,1)S(1)} %fusion.56), channel_id=1, source_target_pairs={{0,64},{16,80},{32,96},{48,112},{64,0},{80,16},{96,32},{112,48},{1... | collective-permute-start | bytes 1032200 | tf_op jit(solution)/shard_map/ppermute | solution.py:28
  104.5 10.5 %collective-permute-start.12 = (bf16[12,48,256]{2,1,0:T(8,128)(2,1)S(1)}, bf16[12,48,256]{2,1,0:T(8,128)(2,1)S(1)}, u32[]{:S(2)}, u32[]{:S(2)}) collective-permute-start(bf16[12,48,256]{2,1,0:T(8,128)(2,1)S(1)} %fusion.62), channel_id=1, source_target_pairs={{0,4},{1,5},{2,6},{3,7},{4,0},{5,1},{6,2},{7,3},{8,12},{9,13},{10,... | collective-permute-start | bytes 884744 | tf_op jit(solution)/shard_map/ppermute | solution.py:37
  104.6 10.5 %collective-permute-start.13 = (bf16[12,48,256]{2,1,0:T(8,128)(2,1)S(1)}, bf16[12,48,256]{2,1,0:T(8,128)(2,1)S(1)}, u32[]{:S(2)}, u32[]{:S(2)}) collective-permute-start(bf16[12,48,256]{2,1,0:T(8,128)(2,1)S(1)} %fusion.62), channel_id=1, source_target_pairs={{0,12},{1,13},{2,14},{3,15},{4,8},{5,9},{6,10},{7,11},{8,4},{9,5},... | collective-permute-start | bytes 884744 | tf_op jit(solution)/shard_map/ppermute | solution.py:37
  106.5 9.3 %collective-permute-start.14 = (bf16[12,48,256]{2,1,0:T(8,128)(2,1)S(1)}, bf16[12,48,256]{2,1,0:T(8,128)(2,1)S(1)}, u32[]{:S(2)}, u32[]{:S(2)}) collective-permute-start(bf16[12,48,256]{2,1,0:T(8,128)(2,1)S(1)} %fusion.62), channel_id=1, source_target_pairs={{0,8},{1,9},{2,10},{3,11},{4,12},{5,13},{6,14},{7,15},{8,0},{9,1},... | collective-permute-start | bytes 884744 | tf_op jit(solution)/shard_map/ppermute | solution.py:37
  107.9 30.1 %collective-permute-start.24 = (bf16[12,46,256]{2,1,0:T(8,128)(2,1)S(1)}, bf16[12,46,256]{2,1,0:T(8,128)(2,1)S(1)}, u32[]{:S(2)}, u32[]{:S(2)}) collective-permute-start(bf16[12,46,256]{2,1,0:T(8,128)(2,1)S(1)} %fusion.59), channel_id=1, source_target_pairs={{0,4},{1,5},{2,6},{3,7},{4,0},{5,1},{6,2},{7,3},{8,12},{9,13},{10,... | collective-permute-start | bytes 847880 | tf_op jit(solution)/shard_map/ppermute | solution.py:37
  112.4 25.6 %collective-permute-start.25 = (bf16[12,46,256]{2,1,0:T(8,128)(2,1)S(1)}, bf16[12,46,256]{2,1,0:T(8,128)(2,1)S(1)}, u32[]{:S(2)}, u32[]{:S(2)}) collective-permute-start(bf16[12,46,256]{2,1,0:T(8,128)(2,1)S(1)} %fusion.59), channel_id=1, source_target_pairs={{0,12},{1,13},{2,14},{3,15},{4,8},{5,9},{6,10},{7,11},{8,4},{9,5},... | collective-permute-start | bytes 847880 | tf_op jit(solution)/shard_map/ppermute | solution.py:37
  115.0 14.4 %collective-permute-start.20 = (bf16[12,56,256]{2,1,0:T(8,128)(2,1)S(1)}, bf16[12,56,256]{2,1,0:T(8,128)(2,1)S(1)}, u32[]{:S(2)}, u32[]{:S(2)}) collective-permute-start(bf16[12,56,256]{2,1,0:T(8,128)(2,1)S(1)} %fusion.55), channel_id=1, source_target_pairs={{0,4},{1,5},{2,6},{3,7},{4,0},{5,1},{6,2},{7,3},{8,12},{9,13},{10,... | collective-permute-start | bytes 1032200 | tf_op jit(solution)/shard_map/ppermute | solution.py:37
  115.1 21.5 %collective-permute-start.21 = (bf16[12,56,256]{2,1,0:T(8,128)(2,1)S(1)}, bf16[12,56,256]{2,1,0:T(8,128)(2,1)S(1)}, u32[]{:S(2)}, u32[]{:S(2)}) collective-permute-start(bf16[12,56,256]{2,1,0:T(8,128)(2,1)S(1)} %fusion.55), channel_id=1, source_target_pairs={{0,12},{1,13},{2,14},{3,15},{4,8},{5,9},{6,10},{7,11},{8,4},{9,5},... | collective-permute-start | bytes 1032200 | tf_op jit(solution)/shard_map/ppermute | solution.py:37
  115.8 21.1 %collective-permute-start.22 = (bf16[12,56,256]{2,1,0:T(8,128)(2,1)S(1)}, bf16[12,56,256]{2,1,0:T(8,128)(2,1)S(1)}, u32[]{:S(2)}, u32[]{:S(2)}) collective-permute-start(bf16[12,56,256]{2,1,0:T(8,128)(2,1)S(1)} %fusion.55), channel_id=1, source_target_pairs={{0,8},{1,9},{2,10},{3,11},{4,12},{5,13},{6,14},{7,15},{8,0},{9,1},... | collective-permute-start | bytes 1032200 | tf_op jit(solution)/shard_map/ppermute | solution.py:37
  129.4 14.1 %collective-permute-start.26 = (bf16[12,46,256]{2,1,0:T(8,128)(2,1)S(1)}, bf16[12,46,256]{2,1,0:T(8,128)(2,1)S(1)}, u32[]{:S(2)}, u32[]{:S(2)}) collective-permute-start(bf16[12,46,256]{2,1,0:T(8,128)(2,1)S(1)} %fusion.59), channel_id=1, source_target_pairs={{0,8},{1,9},{2,10},{3,11},{4,12},{5,13},{6,14},{7,15},{8,0},{9,1},... | collective-permute-start | bytes 847880 | tf_op jit(solution)/shard_map/ppermute | solution.py:37
  145.1 30.3 %copy-start.5 = (s32[256]{0:T(256)S(1)}, s32[256]{0:T(256)}, u32[]{:S(2)}) copy-start(s32[256]{0:T(256)} %param.7) | copy-start | bytes 3076
  145.1 9.1 %collective-permute-start.27 = (bf16[12,288,256]{2,1,0:T(8,128)(2,1)S(1)}, bf16[12,288,256]{2,1,0:T(8,128)(2,1)S(1)}, u32[]{:S(2)}, u32[]{:S(2)}) collective-permute-start(bf16[12,288,256]{2,1,0:T(8,128)(2,1)S(1)} %slice.328), channel_id=1, source_target_pairs={{0,1},{1,0},{2,3},{3,2},{4,5},{5,4},{6,7},{7,6},{8,9},{9,8},{10,11... | collective-permute-start | bytes 5308424 | tf_op jit(solution)/shard_map/ppermute | solution.py:97
  154.3 22.7 %copy-start.1 = (bf16[150,2304]{1,0:T(8,128)(2,1)S(1)}, bf16[150,2304]{1,0:T(8,128)(2,1)}, u32[]{:S(2)}) copy-start(bf16[150,2304]{1,0:T(8,128)(2,1)} %param.6) | copy-start | bytes 2073604
  154.6 20.9 %collective-permute-start.28 = (bf16[12,144,256]{2,1,0:T(8,128)(2,1)S(1)}, bf16[12,144,256]{2,1,0:T(8,128)(2,1)S(1)}, u32[]{:S(2)}, u32[]{:S(2)}) collective-permute-start(bf16[12,144,256]{2,1,0:T(8,128)(2,1)S(1)} %fusion.9), channel_id=1, source_target_pairs={{0,2},{1,3},{2,0},{3,1},{4,6},{5,7},{6,4},{7,5},{8,10},{9,11},{10,... | collective-permute-start | bytes 2654216 | tf_op jit(solution)/shard_map/ppermute | solution.py:98
  (5 other events, 28.0 us)

commit v4 on v3

--- a/solution.py
+++ b/solution.py
@@ -41,19 +41,21 @@
     return v.astype(F32)
 
 
-def x_first(d, cols):
+def x_first(d, cols, later=()):
     a1 = row(d[2 * B : 6 * B, :, :H], 1)
     b1 = row(d[4 * B :, :, H:], 3)
     da, a1 = lax.optimization_barrier((d, a1))
     a2 = row((f32(da[6 * B :, :, :H]) + a1[2 * B :]).astype(BF16), 3)
     db, b1 = lax.optimization_barrier((d, b1))
-    b2 = row((f32(db[2 * B : 4 * B, :, H:]) + b1[: 2 * B]).astype(BF16), 1)
+    sb = (f32(db[2 * B : 4 * B, :, H:]) + b1[: 2 * B]).astype(BF16)
+    sb, *later = lax.optimization_barrier((sb, *later))
+    b2 = row(sb, 1)
     d, a2, b2, *cols = lax.optimization_barrier((d, a2, b2, *cols))
     own = jnp.concatenate(
         [f32(d[: 2 * B, :, :H]) + a1[: 2 * B] + a2, f32(d[: 2 * B, :, H:]) + b1[2 * B :] + b2], axis=2
     )
     y = row(own[B:].astype(BF16), 4)
-    return (own[:B] + y).astype(BF16), *cols
+    return (own[:B] + y).astype(BF16), cols, later
 
 
 def local(integrals, occ_coef, virt_coef, pair_index):
@@ -71,7 +73,9 @@
         weights = lax.optimization_barrier((occ, held))[0]
         d = jnp.einsum("mi,mnp->inp", weights, integrals[:, lo:hi], preferred_element_type=F32).astype(BF16)
         products[name] = held = rowmajor(d)
-    products["r"], virt_coef, _ = lax.optimization_barrier((products["r"], virt_coef, held))
+    products["r"], _ = lax.optimization_barrier((products["r"], held))
+    halves = {}
+    halves["p"], _, (virt_coef, products["q"]) = x_first(products["p"], [], [virt_coef, products["q"]])
 
     apos = jnp.arange(4 * A_BLK, dtype=jnp.int32)
     a_source = ((yl ^ ((apos // A_BLK) % 2)) * 2 + (core ^ (apos // (2 * A_BLK)))) * A_BLK + apos % A_BLK
@@ -83,13 +87,9 @@
 
     cols = {n: jnp.concatenate([virt[k][lo:hi] for k in (0, 1, 3, 2)], axis=0) for n, (lo, hi) in CHUNKS.items()}
 
-    halves = {}
-    for name, d in products.items():
-        if name == "q":
-            halves[name], *tied = x_first(d, list(cols.values()))
-            cols = dict(zip(cols, tied))
-        else:
-            halves[name] = x_first(d, [])[0]
+    halves["r"] = x_first(products["r"], [])[0]
+    halves["q"], tied, _ = x_first(products["q"], list(cols.values()))
+    cols = dict(zip(cols, tied))
     acc = 0.0
     for name, half in halves.items():
         acc = acc + jnp.einsum("inp,na->iap", gather_z(half), cols[name], preferred_element_type=F32)

time: 178 us -> 174 us (0.978)
  local copies, waits for them, and re-layouts: 29.4 us -> 17.4 us
  other arithmetic: 2 us -> 8.46 us
  matrix products: 20.1 us -> 15.8 us
  waiting for transfers between devices: 81.4 us -> 85.4 us
  starting transfers between devices: 43.6 us -> 46 us
    ppermute x15, waiting for transfers between devices: 35.8 us -> 44.3 us  [row(): return lax.ppermute(v, 'row', row_perm(mask))]
    slice x12 -> x15, local copies, waits for them, and re-layouts: 7.7 us -> 0.08 us  [local(): virt[k][lo:hi]]
    ppermute x9, waiting for transfers between devices: 22.7 us -> 18.4 us  [gather_z(): lax.ppermute(half, 'col', col_xor(4 * k))]
    dot_general x3, matrix products: 10.8 us -> 7.63 us  [local(): jnp.einsum('mi,mnp->inp', weights, integrals[:, lo:hi], preferred_element...]
    ppermute x3, starting transfers between devices: 5.77 us -> 8.11 us  [local(): virt[k] = v if k == 0 else lax.ppermute(v, 'col', col_xor(4 * k))]
    add x3, other arithmetic: 0.63 us -> 2.97 us  [x_first(): f32(d[:2 * B, :, H:]) + b1[2 * B:] + b2]
    convert_element_type x6, other arithmetic: 0.51 us -> 2.67 us  [the longest x3 2.45 us: x_first(): sb = (f32(db[2 * B:4 * B, :, H:]) + b1[:2 * B]).astype(BF16)]
    convert_element_type x3, other arithmetic: 0.27 us -> 2.3 us  [x_first(): a2 = row((f32(da[6 * B:, :, :H]) + a1[2 * B:]).astype(BF16), 3)]
  transfers between devices with their start and end apart: 29 -> 29, of which waited for: 12 -> 12; matrix products, arithmetic and copies ran while one was open for 12% -> 14% of each run, Pallas kernels for 0% -> 0%
where the time goes in v4:
time: 174 us
  waiting for transfers between devices  85.4 us (49%)
  starting transfers between devices  46 us (26%)
  local copies, waits for them, and re-layouts  17.4 us (10%)
  matrix products  15.8 us (9%)
  other arithmetic  8.46 us (5%)
    ppermute x15, waiting for transfers between devices, row(): return lax.ppermute(v, 'row', row_perm(mask))  44.3 us
    ppermute x1, waiting for transfers between devices, local(): lax.ppermute((acc[:, A_BLK:2 * A_BLK] + r4[:, A_BLK:]).astype(BF16), 'col...  19.5 us
    ppermute x15, starting transfers between devices, row(): return lax.ppermute(v, 'row', row_perm(mask))  19.2 us
    ppermute x9, waiting for transfers between devices, gather_z(): lax.ppermute(half, 'col', col_xor(4 * k))  18.4 us
    ppermute x9, starting transfers between devices, gather_z(): lax.ppermute(half, 'col', col_xor(4 * k))  11.1 us
    ppermute x3, starting transfers between devices, local(): virt[k] = v if k == 0 else lax.ppermute(v, 'col', col_xor(4 * k))  8.11 us
    dot_general x3, matrix products, local(): jnp.einsum('mi,mnp->inp', weights, integrals[:, lo:hi], preferred_element...  7.63 us
    slice x6, local copies, waits for them, and re-layouts, local(): integrals[:, lo:hi]  6.65 us
  transfers between devices with their start and end apart: 29, of which 12 were waited for; matrix products, arithmetic and copies ran while one was open for 14% of the time, Pallas kernels for 0%

profile of v4, /device:TPU:1, one launch (start us, length us, event | category | flops | bytes accessed | tf_op | source)
XLA Modules:
  0.0 173.6 jit_solution(17363321846143360601)
XLA Ops:
  1.2 3.1 %slice-done = bf16[300,48,256]{2,1,0:T(8,128)(2,1)S(1)} async-done(((bf16[300,150,256]{2,1,0:T(8,128)(2,1)}), bf16[300,48,256]{2,1,0:T(8,128)(2,1)S(1)}, s32[]{:S(2)}) %slice-start) | async-done | bytes 7372824 | tf_op jit(solution)/shard_map/slice | solution.py:74
  4.3 2.7 %fusion.2 = bf16[96,48,256]{2,0,1:T(8,128)(2,1)S(1)} fusion(bf16[300,48,256]{2,1,0:T(8,128)(2,1)S(1)} %slice-done, bf16[300,96]{0,1:T(8,128)(2,1)S(1)} %fusion.46), kind=kOutput, calls=%fused_computation.2 | convolution fusion | flops 707788800 | bytes 9789696 | tf_op jit(solution)/shard_map/mi,mnp->inp/dot_general | solution.py:74
  11.2 3.3 %collective-permute-start = (bf16[48,48,128]{2,1,0:T(8,128)(2,1)}, bf16[48,48,128]{2,1,0:T(8,128)(2,1)}, u32[]{:S(2)}, u32[]{:S(2)}) collective-permute-start(bf16[48,48,128]{2,1,0:T(8,128)(2,1)} %get-tuple-element.77), channel_id=1, source_target_pairs={{0,48},{16,32},{32,16},{48,0},{64,112},{80,96},{96,80},{112,64},{1... | collective-permute-start | bytes 1769480 | tf_op jit(solution)/shard_map/ppermute | solution.py:28
  14.5 3.5 %slice-done.1 = bf16[300,56,256]{2,1,0:T(8,128)(2,1)S(1)} async-done(((bf16[300,150,256]{2,1,0:T(8,128)(2,1)}), bf16[300,56,256]{2,1,0:T(8,128)(2,1)S(1)}, s32[]{:S(2)}) %slice-start.1) | async-done | bytes 8601624 | tf_op jit(solution)/shard_map/slice | solution.py:74
  18.0 2.2 %fusion = bf16[96,56,256]{2,0,1:T(8,128)(2,1)S(1)} fusion(bf16[300,56,256]{2,1,0:T(8,128)(2,1)S(1)} %slice-done.1, bf16[300,96]{0,1:T(8,128)(2,1)S(1)} %fusion.46), kind=kOutput, calls=%fused_computation | convolution fusion | flops 825753600 | bytes 11411712 | tf_op jit(solution)/shard_map/mi,mnp->inp/dot_general | solution.py:74
  20.1 1.6 copy.48
  21.7 2.7 %fusion.6 = bf16[96,46,256]{2,0,1:T(8,128)(2,1)S(1)} fusion(bf16[300,46,256]{2,1,0:T(8,128)(2,1)S(1)} %slice-done.2, bf16[300,96]{0,1:T(8,128)(2,1)S(1)} %fusion.46), kind=kOutput, calls=%fused_computation.10 | convolution fusion | flops 679428096 | bytes 9384192 | tf_op jit(solution)/shard_map/mi,mnp->inp/dot_general | solution.py:74
  24.4 2.7 %copy.28 = bf16[96,46,256]{2,1,0:T(8,128)(2,1)} copy(bf16[96,46,256]{2,0,1:T(8,128)(2,1)S(1)} %fusion.6) | data formatting | bytes 4521984 | tf_op jit(solution)/shard_map/convert_element_type | solution.py:74
  32.3 1.9 %collective-permute-start.5 = (bf16[150,576]{1,0:T(8,128)(2,1)S(1)}, bf16[150,576]{1,0:T(8,128)(2,1)S(1)}, u32[]{:S(2)}, u32[]{:S(2)}) collective-permute-start(bf16[150,576]{1,0:T(8,128)(2,1)S(1)} %fusion.33), channel_id=1, source_target_pairs={{0,4},{1,5},{2,6},{3,7},{4,0},{5,1},{6,2},{7,3},{8,12},{9,13},{10,... | collective-permute-start | bytes 518408 | tf_op jit(solution)/shard_map/ppermute | solution.py:86
  34.7 2.3 %collective-permute-start.6 = (bf16[150,576]{1,0:T(8,128)(2,1)S(1)}, bf16[150,576]{1,0:T(8,128)(2,1)S(1)}, u32[]{:S(2)}, u32[]{:S(2)}) collective-permute-start(bf16[150,576]{1,0:T(8,128)(2,1)S(1)} %fusion.34), channel_id=1, source_target_pairs={{0,12},{1,13},{2,14},{3,15},{4,8},{5,9},{6,10},{7,11},{8,4},{9,5},... | collective-permute-start | bytes 518408 | tf_op jit(solution)/shard_map/ppermute | solution.py:86
  38.1 19.0 %collective-permute-done.8 = bf16[48,48,128]{2,1,0:T(8,128)(2,1)} collective-permute-done((bf16[48,48,128]{2,1,0:T(8,128)(2,1)}, bf16[48,48,128]{2,1,0:T(8,128)(2,1)}, u32[]{:S(2)}, u32[]{:S(2)}) %collective-permute-start.8) | collective-permute-done | bytes 589856 | tf_op jit(solution)/shard_map/ppermute | solution.py:28
  57.1 3.9 %collective-permute-start.7 = (bf16[150,576]{1,0:T(8,128)(2,1)S(1)}, bf16[150,576]{1,0:T(8,128)(2,1)S(1)}, u32[]{:S(2)}, u32[]{:S(2)}) collective-permute-start(bf16[150,576]{1,0:T(8,128)(2,1)S(1)} %fusion.35), channel_id=1, source_target_pairs={{0,8},{1,9},{2,10},{3,11},{4,12},{5,13},{6,14},{7,15},{8,0},{9,1},... | collective-permute-start | bytes 518408 | tf_op jit(solution)/shard_map/ppermute | solution.py:86
  62.1 2.6 %collective-permute-start.3 = (bf16[48,46,128]{2,0,1:T(8,128)(2,1)S(1)}, bf16[48,46,128]{2,0,1:T(8,128)(2,1)S(1)}, u32[]{:S(2)}, u32[]{:S(2)}) collective-permute-start(bf16[48,46,128]{2,0,1:T(8,128)(2,1)S(1)} %copy.31), channel_id=1, source_target_pairs={{0,48},{16,32},{32,16},{48,0},{64,112},{80,96},{96,80},{112,64},{1... | collective-permute-start | bytes 1695752 | tf_op jit(solution)/shard_map/ppermute | solution.py:28
  67.0 1.5 collective-permute-start.10
  69.2 14.7 %collective-permute-done.10 = bf16[24,48,128]{2,1,0:T(8,128)(2,1)S(1)} collective-permute-done((bf16[24,48,128]{2,1,0:T(8,128)(2,1)S(1)}, bf16[24,48,128]{2,1,0:T(8,128)(2,1)S(1)}, u32[]{:S(2)}, u32[]{:S(2)}) %collective-permute-start.10) | collective-permute-done | bytes 294944 | tf_op jit(solution)/shard_map/ppermute | solution.py:28
  85.6 3.0 %collective-permute-start.11 = (bf16[12,48,256]{2,1,0:T(8,128)(2,1)S(1)}, bf16[12,48,256]{2,1,0:T(8,128)(2,1)S(1)}, u32[]{:S(2)}, u32[]{:S(2)}) collective-permute-start(bf16[12,48,256]{2,1,0:T(8,128)(2,1)S(1)} %fusion.64), channel_id=1, source_target_pairs={{0,64},{16,80},{32,96},{48,112},{64,0},{80,16},{96,32},{112,48},{1... | collective-permute-start | bytes 884744 | tf_op jit(solution)/shard_map/ppermute | solution.py:28
  88.5 2.7 %collective-permute-done.18 = bf16[24,56,128]{2,1,0:T(8,128)(2,1)S(1)} collective-permute-done((bf16[24,56,128]{2,1,0:T(8,128)(2,1)S(1)}, bf16[24,56,128]{2,1,0:T(8,128)(2,1)S(1)}, u32[]{:S(2)}, u32[]{:S(2)}) %collective-permute-start.18) | collective-permute-done | bytes 344096 | tf_op jit(solution)/shard_map/ppermute | solution.py:28
  92.6 3.0 %collective-permute-start.19 = (bf16[12,56,256]{2,1,0:T(8,128)(2,1)S(1)}, bf16[12,56,256]{2,1,0:T(8,128)(2,1)S(1)}, u32[]{:S(2)}, u32[]{:S(2)}) collective-permute-start(bf16[12,56,256]{2,1,0:T(8,128)(2,1)S(1)} %fusion.56), channel_id=1, source_target_pairs={{0,64},{16,80},{32,96},{48,112},{64,0},{80,16},{96,32},{112,48},{1... | collective-permute-start | bytes 1032200 | tf_op jit(solution)/shard_map/ppermute | solution.py:28
  97.8 5.7 %collective-permute-done.19 = bf16[12,56,256]{2,1,0:T(8,128)(2,1)S(1)} collective-permute-done((bf16[12,56,256]{2,1,0:T(8,128)(2,1)S(1)}, bf16[12,56,256]{2,1,0:T(8,128)(2,1)S(1)}, u32[]{:S(2)}, u32[]{:S(2)}) %collective-permute-start.19) | collective-permute-done | bytes 344096 | tf_op jit(solution)/shard_map/ppermute | solution.py:28
  104.7 2.2 %collective-permute-start.21 = (bf16[12,56,256]{2,1,0:T(8,128)(2,1)S(1)}, bf16[12,56,256]{2,1,0:T(8,128)(2,1)S(1)}, u32[]{:S(2)}, u32[]{:S(2)}) collective-permute-start(bf16[12,56,256]{2,1,0:T(8,128)(2,1)S(1)} %fusion.55), channel_id=1, source_target_pairs={{0,12},{1,13},{2,14},{3,15},{4,8},{5,9},{6,10},{7,11},{8,4},{9,5},... | collective-permute-start | bytes 1032200 | tf_op jit(solution)/shard_map/ppermute | solution.py:37
  108.4 2.9 %collective-permute-start.23 = (bf16[12,46,256]{2,1,0:T(8,128)(2,1)S(1)}, bf16[12,46,256]{2,1,0:T(8,128)(2,1)S(1)}, u32[]{:S(2)}, u32[]{:S(2)}) collective-permute-start(bf16[12,46,256]{2,1,0:T(8,128)(2,1)S(1)} %fusion.63), channel_id=1, source_target_pairs={{0,64},{16,80},{32,96},{48,112},{64,0},{80,16},{96,32},{112,48},{1... | collective-permute-start | bytes 847880 | tf_op jit(solution)/shard_map/ppermute | solution.py:28
  113.7 2.1 %collective-permute-done.23 = bf16[12,46,256]{2,1,0:T(8,128)(2,1)S(1)} collective-permute-done((bf16[12,46,256]{2,1,0:T(8,128)(2,1)S(1)}, bf16[12,46,256]{2,1,0:T(8,128)(2,1)S(1)}, u32[]{:S(2)}, u32[]{:S(2)}) %collective-permute-start.23) | collective-permute-done | bytes 282656 | tf_op jit(solution)/shard_map/ppermute | solution.py:28
  115.9 2.4 %collective-permute-start.25 = (bf16[12,46,256]{2,1,0:T(8,128)(2,1)S(1)}, bf16[12,46,256]{2,1,0:T(8,128)(2,1)S(1)}, u32[]{:S(2)}, u32[]{:S(2)}) collective-permute-start(bf16[12,46,256]{2,1,0:T(8,128)(2,1)S(1)} %fusion.59), channel_id=1, source_target_pairs={{0,12},{1,13},{2,14},{3,15},{4,8},{5,9},{6,10},{7,11},{8,4},{9,5},... | collective-permute-start | bytes 847880 | tf_op jit(solution)/shard_map/ppermute | solution.py:37
  118.3 3.4 %collective-permute-start.26 = (bf16[12,46,256]{2,1,0:T(8,128)(2,1)S(1)}, bf16[12,46,256]{2,1,0:T(8,128)(2,1)S(1)}, u32[]{:S(2)}, u32[]{:S(2)}) collective-permute-start(bf16[12,46,256]{2,1,0:T(8,128)(2,1)S(1)} %fusion.59), channel_id=1, source_target_pairs={{0,8},{1,9},{2,10},{3,11},{4,12},{5,13},{6,14},{7,15},{8,0},{9,1},... | collective-permute-start | bytes 847880 | tf_op jit(solution)/shard_map/ppermute | solution.py:37
  121.7 5.9 %collective-permute-done.22 = bf16[12,56,256]{2,1,0:T(8,128)(2,1)S(1)} collective-permute-done((bf16[12,56,256]{2,1,0:T(8,128)(2,1)S(1)}, bf16[12,56,256]{2,1,0:T(8,128)(2,1)S(1)}, u32[]{:S(2)}, u32[]{:S(2)}) %collective-permute-start.22) | collective-permute-done | bytes 344096 | tf_op jit(solution)/shard_map/ppermute | solution.py:37
  128.7 1.5 collective-permute-done.24
  130.2 2.5 %collective-permute-done.25 = bf16[12,46,256]{2,1,0:T(8,128)(2,1)S(1)} collective-permute-done((bf16[12,46,256]{2,1,0:T(8,128)(2,1)S(1)}, bf16[12,46,256]{2,1,0:T(8,128)(2,1)S(1)}, u32[]{:S(2)}, u32[]{:S(2)}) %collective-permute-start.25) | collective-permute-done | bytes 282656 | tf_op jit(solution)/shard_map/ppermute | solution.py:37
  132.7 7.2 %collective-permute-done.26 = bf16[12,46,256]{2,1,0:T(8,128)(2,1)S(1)} collective-permute-done((bf16[12,46,256]{2,1,0:T(8,128)(2,1)S(1)}, bf16[12,46,256]{2,1,0:T(8,128)(2,1)S(1)}, u32[]{:S(2)}, u32[]{:S(2)}) %collective-permute-start.26) | collective-permute-done | bytes 282656 | tf_op jit(solution)/shard_map/ppermute | solution.py:37
  141.6 6.1 %collective-permute-start.27 = (bf16[12,288,256]{2,1,0:T(8,128)(2,1)S(1)}, bf16[12,288,256]{2,1,0:T(8,128)(2,1)S(1)}, u32[]{:S(2)}, u32[]{:S(2)}) collective-permute-start(bf16[12,288,256]{2,1,0:T(8,128)(2,1)S(1)} %slice.326), channel_id=1, source_target_pairs={{0,1},{1,0},{2,3},{3,2},{4,5},{5,4},{6,7},{7,6},{8,9},{9,8},{10,11... | collective-permute-start | bytes 5308424 | tf_op jit(solution)/shard_map/ppermute | solution.py:97
  147.7 3.3 %collective-permute-done.27 = bf16[12,288,256]{2,1,0:T(8,128)(2,1)S(1)} collective-permute-done((bf16[12,288,256]{2,1,0:T(8,128)(2,1)S(1)}, bf16[12,288,256]{2,1,0:T(8,128)(2,1)S(1)}, u32[]{:S(2)}, u32[]{:S(2)}) %collective-permute-start.27) | collective-permute-done | bytes 1769504 | tf_op jit(solution)/shard_map/ppermute | solution.py:97
  151.3 1.5 collective-permute-start.28
  152.7 19.5 %collective-permute-done.28 = bf16[12,144,256]{2,1,0:T(8,128)(2,1)S(1)} collective-permute-done((bf16[12,144,256]{2,1,0:T(8,128)(2,1)S(1)}, bf16[12,144,256]{2,1,0:T(8,128)(2,1)S(1)}, u32[]{:S(2)}, u32[]{:S(2)}) %collective-permute-start.28) | collective-permute-done | bytes 884768 | tf_op jit(solution)/shard_map/ppermute | solution.py:98
  (103 shorter events, 30.5 us)
Async XLA Ops:
  0.0 31.3 %copy-start = (bf16[150,2304]{1,0:T(8,128)(2,1)S(1)}, bf16[150,2304]{1,0:T(8,128)(2,1)}, u32[]{:S(2)}) copy-start(bf16[150,2304]{1,0:T(8,128)(2,1)} %param.6) | copy-start | bytes 2073604
  11.2 18.8 %collective-permute-start = (bf16[48,48,128]{2,1,0:T(8,128)(2,1)}, bf16[48,48,128]{2,1,0:T(8,128)(2,1)}, u32[]{:S(2)}, u32[]{:S(2)}) collective-permute-start(bf16[48,48,128]{2,1,0:T(8,128)(2,1)} %get-tuple-element.77), channel_id=1, source_target_pairs={{0,48},{16,32},{32,16},{48,0},{64,112},{80,96},{96,80},{112,64},{1... | collective-permute-start | bytes 1769480 | tf_op jit(solution)/shard_map/ppermute | solution.py:28
  28.5 33.6 %collective-permute-start.17 = (bf16[48,56,128]{2,1,0:T(8,128)(2,1)}, bf16[48,56,128]{2,1,0:T(8,128)(2,1)}, u32[]{:S(2)}, u32[]{:S(2)}) collective-permute-start(bf16[48,56,128]{2,1,0:T(8,128)(2,1)} %get-tuple-element.69), channel_id=1, source_target_pairs={{0,48},{16,32},{32,16},{48,0},{64,112},{80,96},{96,80},{112,64},{1... | collective-permute-start | bytes 2064392 | tf_op jit(solution)/shard_map/ppermute | solution.py:28
  28.5 37.3 %collective-permute-start.15 = (bf16[48,56,128]{2,1,0:T(8,128)(2,1)}, bf16[48,56,128]{2,1,0:T(8,128)(2,1)}, u32[]{:S(2)}, u32[]{:S(2)}) collective-permute-start(bf16[48,56,128]{2,1,0:T(8,128)(2,1)} %get-tuple-element.70), channel_id=1, source_target_pairs={{0,16},{16,0},{32,48},{48,32},{64,80},{80,64},{96,112},{112,96},{1... | collective-permute-start | bytes 2064392 | tf_op jit(solution)/shard_map/ppermute | solution.py:28
  28.7 28.4 %collective-permute-start.8 = (bf16[48,48,128]{2,1,0:T(8,128)(2,1)}, bf16[48,48,128]{2,1,0:T(8,128)(2,1)}, u32[]{:S(2)}, u32[]{:S(2)}) collective-permute-start(bf16[48,48,128]{2,1,0:T(8,128)(2,1)} %get-tuple-element.78), channel_id=1, source_target_pairs={{0,16},{16,0},{32,48},{48,32},{64,80},{80,64},{96,112},{112,96},{1... | collective-permute-start | bytes 1769480 | tf_op jit(solution)/shard_map/ppermute | solution.py:28
  32.3 34.7 %collective-permute-start.5 = (bf16[150,576]{1,0:T(8,128)(2,1)S(1)}, bf16[150,576]{1,0:T(8,128)(2,1)S(1)}, u32[]{:S(2)}, u32[]{:S(2)}) collective-permute-start(bf16[150,576]{1,0:T(8,128)(2,1)S(1)} %fusion.33), channel_id=1, source_target_pairs={{0,4},{1,5},{2,6},{3,7},{4,0},{5,1},{6,2},{7,3},{8,12},{9,13},{10,... | collective-permute-start | bytes 518408 | tf_op jit(solution)/shard_map/ppermute | solution.py:86
  34.7 33.8 %collective-permute-start.6 = (bf16[150,576]{1,0:T(8,128)(2,1)S(1)}, bf16[150,576]{1,0:T(8,128)(2,1)S(1)}, u32[]{:S(2)}, u32[]{:S(2)}) collective-permute-start(bf16[150,576]{1,0:T(8,128)(2,1)S(1)} %fusion.34), channel_id=1, source_target_pairs={{0,12},{1,13},{2,14},{3,15},{4,8},{5,9},{6,10},{7,11},{8,4},{9,5},... | collective-permute-start | bytes 518408 | tf_op jit(solution)/shard_map/ppermute | solution.py:86
  37.5 31.4 %slice-start.3 = ((bf16[150,576]{1,0:T(8,128)(2,1)}), bf16[46,576]{1,0:T(8,128)(2,1)S(1)}, s32[]{:S(2)}) async-start(bf16[150,576]{1,0:T(8,128)(2,1)} %copy-done.4), calls=%async_computation.3 | async-start | bytes 122880 | tf_op jit(solution)/shard_map/slice | solution.py:88
  38.1 31.1 %slice-start.4 = ((bf16[150,576]{1,0:T(8,128)(2,1)}), bf16[56,576]{1,0:T(8,128)(2,1)S(1)}, s32[]{:S(2)}) async-start(bf16[150,576]{1,0:T(8,128)(2,1)} %copy-done.4), calls=%async_computation.4 | async-start | bytes 143360 | tf_op jit(solution)/shard_map/slice | solution.py:88
  57.1 11.7 %collective-permute-start.7 = (bf16[150,576]{1,0:T(8,128)(2,1)S(1)}, bf16[150,576]{1,0:T(8,128)(2,1)S(1)}, u32[]{:S(2)}, u32[]{:S(2)}) collective-permute-start(bf16[150,576]{1,0:T(8,128)(2,1)S(1)} %fusion.35), channel_id=1, source_target_pairs={{0,8},{1,9},{2,10},{3,11},{4,12},{5,13},{6,14},{7,15},{8,0},{9,1},... | collective-permute-start | bytes 518408 | tf_op jit(solution)/shard_map/ppermute | solution.py:86
  62.1 33.5 %collective-permute-start.3 = (bf16[48,46,128]{2,0,1:T(8,128)(2,1)S(1)}, bf16[48,46,128]{2,0,1:T(8,128)(2,1)S(1)}, u32[]{:S(2)}, u32[]{:S(2)}) collective-permute-start(bf16[48,46,128]{2,0,1:T(8,128)(2,1)S(1)} %copy.31), channel_id=1, source_target_pairs={{0,48},{16,32},{32,16},{48,0},{64,112},{80,96},{96,80},{112,64},{1... | collective-permute-start | bytes 1695752 | tf_op jit(solution)/shard_map/ppermute | solution.py:28
  65.8 30.5 %collective-permute-start.1 = (bf16[48,46,128]{2,0,1:T(8,128)(2,1)S(1)}, bf16[48,46,128]{2,0,1:T(8,128)(2,1)S(1)}, u32[]{:S(2)}, u32[]{:S(2)}) collective-permute-start(bf16[48,46,128]{2,0,1:T(8,128)(2,1)S(1)} %copy.29), channel_id=1, source_target_pairs={{0,16},{16,0},{32,48},{48,32},{64,80},{80,64},{96,112},{112,96},{1... | collective-permute-start | bytes 1695752 | tf_op jit(solution)/shard_map/ppermute | solution.py:28
  67.0 16.9 %collective-permute-start.10 = (bf16[24,48,128]{2,1,0:T(8,128)(2,1)S(1)}, bf16[24,48,128]{2,1,0:T(8,128)(2,1)S(1)}, u32[]{:S(2)}, u32[]{:S(2)}) collective-permute-start(bf16[24,48,128]{2,1,0:T(8,128)(2,1)S(1)} %add_convert_fusion.5), channel_id=1, source_target_pairs={{0,16},{16,0},{32,48},{48,32},{64,80},{80,64},{96,112},{112,96},{1... | collective-permute-start | bytes 884744 | tf_op jit(solution)/shard_map/ppermute | solution.py:28
  68.5 15.6 %collective-permute-start.9 = (bf16[24,48,128]{2,1,0:T(8,128)(2,1)S(1)}, bf16[24,48,128]{2,1,0:T(8,128)(2,1)S(1)}, u32[]{:S(2)}, u32[]{:S(2)}) collective-permute-start(bf16[24,48,128]{2,1,0:T(8,128)(2,1)S(1)} %add_convert_fusion.2), channel_id=1, source_target_pairs={{0,48},{16,32},{32,16},{48,0},{64,112},{80,96},{96,80},{112,64},{1... | collective-permute-start | bytes 884744 | tf_op jit(solution)/shard_map/ppermute | solution.py:28
  68.8 22.5 %collective-permute-start.18 = (bf16[24,56,128]{2,1,0:T(8,128)(2,1)S(1)}, bf16[24,56,128]{2,1,0:T(8,128)(2,1)S(1)}, u32[]{:S(2)}, u32[]{:S(2)}) collective-permute-start(bf16[24,56,128]{2,1,0:T(8,128)(2,1)S(1)} %add_convert_fusion), channel_id=1, source_target_pairs={{0,16},{16,0},{32,48},{48,32},{64,80},{80,64},{96,112},{112,96},{1... | collective-permute-start | bytes 1032200 | tf_op jit(solution)/shard_map/ppermute | solution.py:28
  83.9 7.4 %collective-permute-start.16 = (bf16[24,56,128]{2,1,0:T(8,128)(2,1)S(1)}, bf16[24,56,128]{2,1,0:T(8,128)(2,1)S(1)}, u32[]{:S(2)}, u32[]{:S(2)}) collective-permute-start(bf16[24,56,128]{2,1,0:T(8,128)(2,1)S(1)} %add_convert_fusion.1), channel_id=1, source_target_pairs={{0,48},{16,32},{32,16},{48,0},{64,112},{80,96},{96,80},{112,64},{1... | collective-permute-start | bytes 1032200 | tf_op jit(solution)/shard_map/ppermute | solution.py:28
  85.6 11.4 %collective-permute-start.11 = (bf16[12,48,256]{2,1,0:T(8,128)(2,1)S(1)}, bf16[12,48,256]{2,1,0:T(8,128)(2,1)S(1)}, u32[]{:S(2)}, u32[]{:S(2)}) collective-permute-start(bf16[12,48,256]{2,1,0:T(8,128)(2,1)S(1)} %fusion.64), channel_id=1, source_target_pairs={{0,64},{16,80},{32,96},{48,112},{64,0},{80,16},{96,32},{112,48},{1... | collective-permute-start | bytes 884744 | tf_op jit(solution)/shard_map/ppermute | solution.py:28
  92.6 10.9 %collective-permute-start.19 = (bf16[12,56,256]{2,1,0:T(8,128)(2,1)S(1)}, bf16[12,56,256]{2,1,0:T(8,128)(2,1)S(1)}, u32[]{:S(2)}, u32[]{:S(2)}) collective-permute-start(bf16[12,56,256]{2,1,0:T(8,128)(2,1)S(1)} %fusion.56), channel_id=1, source_target_pairs={{0,64},{16,80},{32,96},{48,112},{64,0},{80,16},{96,32},{112,48},{1... | collective-permute-start | bytes 1032200 | tf_op jit(solution)/shard_map/ppermute | solution.py:28
  95.9 7.7 %collective-permute-start.4 = (bf16[24,46,128]{2,1,0:T(8,128)(2,1)S(1)}, bf16[24,46,128]{2,1,0:T(8,128)(2,1)S(1)}, u32[]{:S(2)}, u32[]{:S(2)}) collective-permute-start(bf16[24,46,128]{2,1,0:T(8,128)(2,1)S(1)} %add_convert_fusion.3), channel_id=1, source_target_pairs={{0,16},{16,0},{32,48},{48,32},{64,80},{80,64},{96,112},{112,96},{1... | collective-permute-start | bytes 847880 | tf_op jit(solution)/shard_map/ppermute | solution.py:28
  96.5 8.2 %collective-permute-start.2 = (bf16[24,46,128]{2,1,0:T(8,128)(2,1)S(1)}, bf16[24,46,128]{2,1,0:T(8,128)(2,1)S(1)}, u32[]{:S(2)}, u32[]{:S(2)}) collective-permute-start(bf16[24,46,128]{2,1,0:T(8,128)(2,1)S(1)} %add_convert_fusion.4), channel_id=1, source_target_pairs={{0,48},{16,32},{32,16},{48,0},{64,112},{80,96},{96,80},{112,64},{1... | collective-permute-start | bytes 847880 | tf_op jit(solution)/shard_map/ppermute | solution.py:28
  97.0 10.2 %collective-permute-start.12 = (bf16[12,48,256]{2,1,0:T(8,128)(2,1)S(1)}, bf16[12,48,256]{2,1,0:T(8,128)(2,1)S(1)}, u32[]{:S(2)}, u32[]{:S(2)}) collective-permute-start(bf16[12,48,256]{2,1,0:T(8,128)(2,1)S(1)} %fusion.62), channel_id=1, source_target_pairs={{0,4},{1,5},{2,6},{3,7},{4,0},{5,1},{6,2},{7,3},{8,12},{9,13},{10,... | collective-permute-start | bytes 884744 | tf_op jit(solution)/shard_map/ppermute | solution.py:37
  97.8 10.5 %collective-permute-start.13 = (bf16[12,48,256]{2,1,0:T(8,128)(2,1)S(1)}, bf16[12,48,256]{2,1,0:T(8,128)(2,1)S(1)}, u32[]{:S(2)}, u32[]{:S(2)}) collective-permute-start(bf16[12,48,256]{2,1,0:T(8,128)(2,1)S(1)} %fusion.62), channel_id=1, source_target_pairs={{0,12},{1,13},{2,14},{3,15},{4,8},{5,9},{6,10},{7,11},{8,4},{9,5},... | collective-permute-start | bytes 884744 | tf_op jit(solution)/shard_map/ppermute | solution.py:37
  103.5 9.0 %collective-permute-start.14 = (bf16[12,48,256]{2,1,0:T(8,128)(2,1)S(1)}, bf16[12,48,256]{2,1,0:T(8,128)(2,1)S(1)}, u32[]{:S(2)}, u32[]{:S(2)}) collective-permute-start(bf16[12,48,256]{2,1,0:T(8,128)(2,1)S(1)} %fusion.62), channel_id=1, source_target_pairs={{0,8},{1,9},{2,10},{3,11},{4,12},{5,13},{6,14},{7,15},{8,0},{9,1},... | collective-permute-start | bytes 884744 | tf_op jit(solution)/shard_map/ppermute | solution.py:37
  103.6 14.6 %collective-permute-start.20 = (bf16[12,56,256]{2,1,0:T(8,128)(2,1)S(1)}, bf16[12,56,256]{2,1,0:T(8,128)(2,1)S(1)}, u32[]{:S(2)}, u32[]{:S(2)}) collective-permute-start(bf16[12,56,256]{2,1,0:T(8,128)(2,1)S(1)} %fusion.55), channel_id=1, source_target_pairs={{0,4},{1,5},{2,6},{3,7},{4,0},{5,1},{6,2},{7,3},{8,12},{9,13},{10,... | collective-permute-start | bytes 1032200 | tf_op jit(solution)/shard_map/ppermute | solution.py:37
  104.7 17.0 %collective-permute-start.21 = (bf16[12,56,256]{2,1,0:T(8,128)(2,1)S(1)}, bf16[12,56,256]{2,1,0:T(8,128)(2,1)S(1)}, u32[]{:S(2)}, u32[]{:S(2)}) collective-permute-start(bf16[12,56,256]{2,1,0:T(8,128)(2,1)S(1)} %fusion.55), channel_id=1, source_target_pairs={{0,12},{1,13},{2,14},{3,15},{4,8},{5,9},{6,10},{7,11},{8,4},{9,5},... | collective-permute-start | bytes 1032200 | tf_op jit(solution)/shard_map/ppermute | solution.py:37
  107.2 20.4 %collective-permute-start.22 = (bf16[12,56,256]{2,1,0:T(8,128)(2,1)S(1)}, bf16[12,56,256]{2,1,0:T(8,128)(2,1)S(1)}, u32[]{:S(2)}, u32[]{:S(2)}) collective-permute-start(bf16[12,56,256]{2,1,0:T(8,128)(2,1)S(1)} %fusion.55), channel_id=1, source_target_pairs={{0,8},{1,9},{2,10},{3,11},{4,12},{5,13},{6,14},{7,15},{8,0},{9,1},... | collective-permute-start | bytes 1032200 | tf_op jit(solution)/shard_map/ppermute | solution.py:37
  108.4 7.4 %collective-permute-start.23 = (bf16[12,46,256]{2,1,0:T(8,128)(2,1)S(1)}, bf16[12,46,256]{2,1,0:T(8,128)(2,1)S(1)}, u32[]{:S(2)}, u32[]{:S(2)}) collective-permute-start(bf16[12,46,256]{2,1,0:T(8,128)(2,1)S(1)} %fusion.63), channel_id=1, source_target_pairs={{0,64},{16,80},{32,96},{48,112},{64,0},{80,16},{96,32},{112,48},{1... | collective-permute-start | bytes 847880 | tf_op jit(solution)/shard_map/ppermute | solution.py:28
  115.8 14.4 %collective-permute-start.24 = (bf16[12,46,256]{2,1,0:T(8,128)(2,1)S(1)}, bf16[12,46,256]{2,1,0:T(8,128)(2,1)S(1)}, u32[]{:S(2)}, u32[]{:S(2)}) collective-permute-start(bf16[12,46,256]{2,1,0:T(8,128)(2,1)S(1)} %fusion.59), channel_id=1, source_target_pairs={{0,4},{1,5},{2,6},{3,7},{4,0},{5,1},{6,2},{7,3},{8,12},{9,13},{10,... | collective-permute-start | bytes 847880 | tf_op jit(solution)/shard_map/ppermute | solution.py:37
  115.9 16.8 %collective-permute-start.25 = (bf16[12,46,256]{2,1,0:T(8,128)(2,1)S(1)}, bf16[12,46,256]{2,1,0:T(8,128)(2,1)S(1)}, u32[]{:S(2)}, u32[]{:S(2)}) collective-permute-start(bf16[12,46,256]{2,1,0:T(8,128)(2,1)S(1)} %fusion.59), channel_id=1, source_target_pairs={{0,12},{1,13},{2,14},{3,15},{4,8},{5,9},{6,10},{7,11},{8,4},{9,5},... | collective-permute-start | bytes 847880 | tf_op jit(solution)/shard_map/ppermute | solution.py:37
  118.3 21.7 %collective-permute-start.26 = (bf16[12,46,256]{2,1,0:T(8,128)(2,1)S(1)}, bf16[12,46,256]{2,1,0:T(8,128)(2,1)S(1)}, u32[]{:S(2)}, u32[]{:S(2)}) collective-permute-start(bf16[12,46,256]{2,1,0:T(8,128)(2,1)S(1)} %fusion.59), channel_id=1, source_target_pairs={{0,8},{1,9},{2,10},{3,11},{4,12},{5,13},{6,14},{7,15},{8,0},{9,1},... | collective-permute-start | bytes 847880 | tf_op jit(solution)/shard_map/ppermute | solution.py:37
  141.6 9.4 %collective-permute-start.27 = (bf16[12,288,256]{2,1,0:T(8,128)(2,1)S(1)}, bf16[12,288,256]{2,1,0:T(8,128)(2,1)S(1)}, u32[]{:S(2)}, u32[]{:S(2)}) collective-permute-start(bf16[12,288,256]{2,1,0:T(8,128)(2,1)S(1)} %slice.326), channel_id=1, source_target_pairs={{0,1},{1,0},{2,3},{3,2},{4,5},{5,4},{6,7},{7,6},{8,9},{9,8},{10,11... | collective-permute-start | bytes 5308424 | tf_op jit(solution)/shard_map/ppermute | solution.py:97
  151.3 20.9 %collective-permute-start.28 = (bf16[12,144,256]{2,1,0:T(8,128)(2,1)S(1)}, bf16[12,144,256]{2,1,0:T(8,128)(2,1)S(1)}, u32[]{:S(2)}, u32[]{:S(2)}) collective-permute-start(bf16[12,144,256]{2,1,0:T(8,128)(2,1)S(1)} %fusion.9), channel_id=1, source_target_pairs={{0,2},{1,3},{2,0},{3,1},{4,6},{5,7},{6,4},{7,5},{8,10},{9,11},{10,... | collective-permute-start | bytes 2654216 | tf_op jit(solution)/shard_map/ppermute | solution.py:98
  (9 other events, 108.6 us)
